TPU v7x, 128 devices: a whole 4x4x4 slice. The times are simulated.
128 devices in a mesh: chain: 16 (over z, y_lo, core), tech: 4 (over x), blk: 2 (over y_hi).
Axes of the slice: x: 4, y: 4 (y_hi: 2, y_lo: 2; y = y_hi * 2 + y_lo), z: 4, core: 2. Of those that a mesh axis runs over, the one named last changes fastest.
Arguments:
- block_inverse: bfloat16 [4, 16, 3072, 3072], P('tech', 'chain', 'blk'), may hold values from -1 to 4.5, as said below
- coupling: bfloat16 [4, 16, 3072, 512], P('tech', 'chain', 'blk'), may hold values from -0.0390625 to 0.0390625
- data_rhs: bfloat16 [4, 16, 3072, 256], P('tech', 'chain', 'blk'), may hold values from -6 to 6
- station_seen: int32 [4, 16, 1024], P('tech', 'chain', 'blk'), may hold values 0 or 1
- shared_inverse: float32 [16, 512, 512], P('chain'), may hold values from -0.05 to 1, as said below
- walk_weight: float32 [512], replicated, may hold values from 0.92 to 1
- shared_rhs: float32 [16, 512, 256], P('chain'), may hold values from -1.2 to 1.2
Outputs:
- coords: float32 [4, 16, 3072, 256], P('tech', 'chain', 'blk')
- shared: float32 [16, 512, 256], P('chain')
Inputs may be any that keep to these rules, and one draw needn't show every extreme that they name: `block_inverse`: each block is symmetric. `shared_inverse`: each block is symmetric.
All inputs are finite; a program needn't handle non-finite values. No bound on the sum of `station_seen` on one device may be relied on, other than what follows from the above.
Results may differ from a plain program's by a relative error of at most 0.004.
Values may be sent and summed in bfloat16 or wider, within the bound.
No kernel may reach another device: no remote copies, remote signals or barrier semaphores. Data moves between devices by JAX's collectives and lax.ppermute only.
A program may use at most 128 MiB of HBM per device.

v0:
```python
import jax
import jax.numpy as jnp
from jax import lax
from jax.experimental.layout import Layout, with_layout_constraint
from jax.sharding import Mesh
from jax.sharding import PartitionSpec as P

CHAIN = ("chain_0", "chain_1", "chain_2")
AXES = ("chain_0", "chain_1", "chain_2", "tech", "blk")
SIZES = (4, 2, 2, 4, 2)
REPLICAS = ("tech", "blk")


def place(z, y, c, t, b):
    index = 0
    for value, size in zip((z, y, c, t, b), SIZES):
        index = index * size + value
    return index


def route(target_of):
    pairs = []
    for z in range(4):
        for y in range(2):
            for c in range(2):
                for t in range(4):
                    for b in range(2):
                        target = target_of(z, y, c, t, b)
                        if target is not None:
                            pairs.append((place(z, y, c, t, b), place(*target)))
    return pairs


BLK_SWAP = route(lambda z, y, c, t, b: (z, y, c, t, 1 - b))
CORE_SWAP = route(lambda z, y, c, t, b: (z, y, 1 - c, t, b))
CHIP_SWAP = route(lambda z, y, c, t, b: (z, 1 - y, c, t, b))
Z_HOPS = [
    route(lambda z, y, c, t, b, h=h: (h, y, c, t, b) if z == h - 1 else None) for h in (1, 2, 3)
]


def week_before(z, y, c, t, b):
    week = (z * 2 + y) * 2 + c - 1
    return None if week < 0 else (week // 4, week // 2 % 2, week % 2, t, b)


LATER = route(week_before)


def moved(value, pairs):
    return lax.ppermute(value, AXES, pairs)


def exact(left, right):
    return jnp.dot(left, right, precision=lax.Precision.HIGH)


def both_halves(own, other, which):
    rows = own.shape[0]
    whole = jnp.zeros((2 * rows, *own.shape[1:]), own.dtype)
    whole = lax.dynamic_update_slice_in_dim(whole, own, which * rows, 0)
    return lax.dynamic_update_slice_in_dim(whole, other, (1 - which) * rows, 0)


def collected(part):
    copies = jnp.broadcast_to(part, (8, *part.shape))
    pieces = lax.all_to_all(copies, REPLICAS, split_axis=0, concat_axis=0, tiled=True)
    return pieces.reshape(8 * part.shape[0], part.shape[1])


def row_major(value):
    return with_layout_constraint(value, Layout(major_to_minor=tuple(range(value.ndim))))


def layer(
    block_inverse, coupling, data_rhs, station_seen, shared_inverse, walk_weight, shared_rhs
):
    replica = lax.axis_index("tech") * 2 + lax.axis_index("blk")
    half = lax.axis_index("blk")
    early_chip = lax.axis_index("chain_1") == 0
    early_core = lax.axis_index("chain_2") == 0

    inverse_rows = block_inverse[0, 0]
    coupling_rows = coupling[0, 0]
    rhs_rows = data_rhs[0, 0]
    station_count = station_seen.shape[2]
    seen_rows = (
        jnp.broadcast_to(station_seen[0, 0][:, None], (station_count, 3))
        .reshape(-1, 1)
        .astype(jnp.float32)
    )
    inverse = shared_inverse[0]
    weight = walk_weight[None, :]
    samples = shared_rhs.shape[2] // 8
    week_rhs = lax.dynamic_slice_in_dim(shared_rhs[0].T, replica * samples, samples, 0)

    rhs_other = moved(rhs_rows, BLK_SWAP)

    step = walk_weight[:, None] * inverse
    step_other = moved(step, CORE_SWAP)
    step_first = jnp.where(early_core, step, step_other)
    step_second = jnp.where(early_core, step_other, step)
    pair = exact(step_first, step_second)
    own_map = jnp.where(early_core, step_first, pair)
    pair_other = moved(pair.astype(jnp.bfloat16), CHIP_SWAP)

    def solved(residual):
        return row_major(
            seen_rows * jnp.dot(inverse_rows, residual, preferred_element_type=jnp.float32)
        )

    def terms_of(coords):
        return lax.dot_general(
            coords.astype(jnp.bfloat16),
            coupling_rows,
            (((0,), (0,)), ((), ())),
            preferred_element_type=jnp.float32,
        ).astype(jnp.bfloat16)

    def summed(terms):
        pieces = lax.all_to_all(
            terms.reshape(8, samples, terms.shape[1]),
            REPLICAS,
            split_axis=0,
            concat_axis=0,
            tiled=True,
        )
        return jnp.sum(pieces.astype(jnp.float32), axis=0)

    def left(rhs, factor, values):
        product = lax.dot_general(
            factor, values, (((1,), (1,)), ((), ())), preferred_element_type=jnp.float32
        )
        return (rhs.astype(jnp.float32) - product).astype(jnp.bfloat16)

    coords = solved(both_halves(rhs_rows, rhs_other, half))
    terms = terms_of(lax.optimization_barrier(coords))
    terms, week_rhs, pair, own_map, step_first, step_second, early_core, early_chip = (
        lax.optimization_barrier(
            (terms, week_rhs, pair, own_map, step_first, step_second, early_core, early_chip)
        )
    )
    station_sum = summed(terms)

    def late_maps(pair_other):
        pair_other = pair_other.astype(jnp.float32)
        pair_first = jnp.where(early_chip, pair, pair_other)
        pair_second = jnp.where(early_chip, pair_other, pair)
        return pair_first, pair_second, exact(pair_first, pair_second)

    def chain(offset, maps):
        pair_first, pair_second, group = maps
        offset_other = moved(offset, CORE_SWAP)
        first = jnp.where(early_core, offset, offset_other)
        second = jnp.where(early_core, offset_other, offset)
        chip_end = second + exact(first, step_second)
        chip_other = moved(chip_end, CHIP_SWAP)
        chip_first = jnp.where(early_chip, chip_end, chip_other)
        chip_second = jnp.where(early_chip, chip_other, chip_end)
        group_end = chip_second + exact(chip_first, pair_second)
        inside = jnp.where(
            early_chip,
            jnp.where(early_core, first, chip_first),
            jnp.where(early_core, first + exact(chip_first, step_first), group_end),
        )
        carried = jnp.zeros_like(offset)
        for hop in Z_HOPS:
            carried = carried + moved(group_end + exact(carried, group), hop)
        entering = jnp.where(early_chip, carried, exact(carried, pair_first))
        return inside + exact(entering, own_map)

    pair_other, station_sum = lax.optimization_barrier((pair_other, station_sum))
    maps = late_maps(pair_other)
    shared = chain(exact(week_rhs - station_sum, inverse), maps)

    shared_low = shared.astype(jnp.bfloat16)
    shared_all = collected(shared_low)
    later = moved(shared_low, LATER).astype(jnp.float32)
    residual_own = left(rhs_rows, coupling_rows, shared_all)
    residual_other = moved(residual_own, BLK_SWAP)
    coords = solved(both_halves(residual_own, residual_other, half))
    station_sum = summed(terms_of(coords))
    shared = chain(exact(week_rhs + weight * later - station_sum, inverse), maps)
    result = collected(shared).T
    return (coords[None, None], result[None])


def solution(mesh):
    layout = Mesh(mesh.devices.reshape(SIZES), AXES)
    return jax.shard_map(
        layer,
        mesh=layout,
        in_specs=(
            P("tech", CHAIN, "blk", None),
            P("tech", CHAIN, "blk", None),
            P("tech", CHAIN, "blk", None),
            P("tech", CHAIN, "blk"),
            P(CHAIN, None, None),
            P(),
            P(CHAIN, None, None),
        ),
        out_specs=(P("tech", CHAIN, "blk", None), P(CHAIN, None, None)),
        check_vma=False,
    )
```

profile of v0, /device:TPU:96, one launch (start us, length us, event | category | flops | bytes accessed | tf_op | source)
XLA Modules:
  0.0 159.0 jit_solution(16126256302016441823)
XLA Ops:
  0.7 1.6 copy.12
  2.2 3.3 %collective-permute-start = (bf16[1536,256]{0,1:T(8,128)(2,1)S(1)}, bf16[1536,256]{0,1:T(8,128)(2,1)}, u32[]{:S(2)}, u32[]{:S(2)}) collective-permute-start(bf16[1536,256]{0,1:T(8,128)(2,1)S(1)} %bitcast.92), channel_id=1, source_target_pairs={{0,1},{1,0},{2,3},{3,2},{4,5},{5,4},{6,7},{7,6},{8,9},{9,8},{10,11... | collective-permute-start | bytes 2359304 | tf_op jit(solution)/shard_map/ppermute | solution.py:51
  5.5 1.1 bitcast_multiply_fusion
  6.6 0.8 broadcast_in_dim.19
  7.5 1.2 convert_element_type.53
  8.6 1.8 %constant_dynamic-slice_fusion = f32[1,512,32]{2,1,0:T(8,128)} fusion(f32[1,512,256]{2,1,0:T(8,128)} %param.13, s32[]{:T(128)S(6)} %select_n.109), kind=kLoop, calls=%fused_computation.66 | loop fusion | bytes 131076 | tf_op jit(solution)/shard_map/dynamic-slice.1
  10.4 1.0 copy.13
  11.8 11.4 %collective-permute-done = bf16[1536,256]{0,1:T(8,128)(2,1)} collective-permute-done((bf16[1536,256]{0,1:T(8,128)(2,1)S(1)}, bf16[1536,256]{0,1:T(8,128)(2,1)}, u32[]{:S(2)}, u32[]{:S(2)}) %collective-permute-start) | collective-permute-done | bytes 786464 | tf_op jit(solution)/shard_map/ppermute | solution.py:51
  23.2 1.2 constant_dynamic-update-slice_fusion.2
  24.4 6.3 %fusion.11 = bf16[1536,256]{1,0:T(8,128)(2,1)S(1)} fusion(bf16[3072,256]{0,1:T(8,128)(2,1)S(1)} %constant_dynamic-update-slice_fusion.2, bf16[1,1,1536,3072]{3,2,1,0:T(8,128)(2,1)} %param.7, f32[1536]{0:T(1024)S(1)} %convert_element_type.53), kind=kOutput, calls=%fused_computation.8 | convolution fusion | flops 2416705536 | bytes 11802624 | tf_op jit(solution)/shard_map/dot_general | solution.py:109
  30.8 1.4 broadcast_select_fusion.1
  32.3 1.1 fusion.50
  33.4 1.7 %collective-permute-start.2 = (bf16[512,512]{1,0:T(8,128)(2,1)S(1)}, bf16[512,512]{1,0:T(8,128)(2,1)S(1)}, u32[]{:S(2)}, u32[]{:S(2)}) collective-permute-start(bf16[512,512]{1,0:T(8,128)(2,1)S(1)} %get-tuple-element.26), channel_id=1, source_target_pairs={{0,16},{1,17},{2,18},{3,19},{4,20},{5,21},{6,22},{7,23},{8,24},{9,... | collective-permute-start | bytes 1572872 | tf_op jit(solution)/shard_map/ppermute | solution.py:51
  35.0 0.6 fusion.20
  35.6 15.9 %all_to_all.20 = bf16[8,32,512]{2,1,0:T(8,128)(2,1)S(1)} all-to-all(bf16[8,32,512]{2,1,0:T(8,128)(2,1)S(1)} %bitcast.96), channel_id=1, replica_groups=mesh['chain_0'=4,'chain_1'=2,'chain_2'=2,'tech'=4,'blk'=2] {'tech','blk'}, dimensions={0} | all-to-all | bytes 524288 | tf_op jit(solution)/shard_map/all_to_all | solution.py:121
  52.1 1.0 fusion.34
  53.3 0.4 select_add_fusion.4
  54.4 3.8 %collective-permute-done.4 = f32[32,512]{1,0:T(8,128)S(1)} collective-permute-done((f32[32,512]{1,0:T(8,128)S(1)}, f32[32,512]{1,0:T(8,128)S(1)}, u32[]{:S(2)}, u32[]{:S(2)}) %collective-permute-start.4) | collective-permute-done | bytes 65568 | tf_op jit(solution)/shard_map/ppermute | solution.py:51
  58.6 0.7 collective-permute-start.5
  59.7 0.7 collective-permute-start.6
  60.8 1.3 collective-permute-start.7
  62.1 11.0 %collective-permute-done.7 = f32[32,512]{1,0:T(8,128)S(1)} collective-permute-done((f32[32,512]{1,0:T(8,128)S(1)}, f32[32,512]{1,0:T(8,128)S(1)}, u32[]{:S(2)}, u32[]{:S(2)}) %collective-permute-start.7) | collective-permute-done | bytes 65568 | tf_op jit(solution)/shard_map/ppermute | solution.py:51
  73.5 0.4 fusion.55
  74.0 0.4 add_convert_fusion
  74.5 12.7 %all_to_all.21 = bf16[8,32,512]{2,1,0:T(8,128)(2,1)S(1)} all-to-all(bf16[8,32,512]{2,1,0:T(8,128)(2,1)S(1)} %broadcast_in_dim.20), channel_id=1, replica_groups=mesh['chain_0'=4,'chain_1'=2,'chain_2'=2,'tech'=4,'blk'=2] {'tech','blk'}, dimensions={0} | all-to-all | bytes 524288 | tf_op jit(solution)/shard_map/all_to_all | solution.py:67
  87.4 0.6 constant_dynamic-update-slice_fusion.1
  88.1 1.5 collective-permute-start.8
  89.5 14.9 %collective-permute-done.8 = bf16[1536,256]{0,1:T(8,128)(2,1)S(1)} collective-permute-done((bf16[1536,256]{0,1:T(8,128)(2,1)S(1)}, bf16[1536,256]{0,1:T(8,128)(2,1)S(1)}, u32[]{:S(2)}, u32[]{:S(2)}) %collective-permute-start.8) | collective-permute-done | bytes 786464 | tf_op jit(solution)/shard_map/ppermute | solution.py:51
  104.5 2.7 %fusion.7 = f32[256,1536]{0,1:T(8,128)S(1)} fusion(bf16[3072,256]{0,1:T(8,128)(2,1)S(1)} %constant_dynamic-update-slice_fusion, bf16[1,1,1536,3072]{3,2,1,0:T(8,128)(2,1)S(1)} %bitcast.102, f32[1536]{0:T(1024)S(1)} %convert_element_type.53), kind=kOutput, calls=%fused_computation.5 | convolution fusion | flops 2416312320 | bytes 12589056 | tf_op jit(solution)/shard_map/dot_general | solution.py:109
  107.2 1.3 fusion.23
  108.5 3.4 %all-to-all-start.2 = ((bf16[8,32,512]{2,1,0:T(8,128)(2,1)}), bf16[8,32,512]{2,1,0:T(8,128)(2,1)S(1)}, u32[]{:S(2)}, u32[]{:S(2)}) async-start(bf16[8,32,512]{2,1,0:T(8,128)(2,1)} %bitcast.97), calls=%async_computation.2 | async-start | bytes 524288 | tf_op jit(solution)/shard_map/all_to_all | solution.py:121
  112.0 1.9 %collective-permute-start.9 = (bf16[32,512]{1,0:T(8,128)(2,1)}, bf16[32,512]{1,0:T(8,128)(2,1)}, u32[]{:S(2)}, u32[]{:S(2)}) collective-permute-start(bf16[32,512]{1,0:T(8,128)(2,1)} %copy-done.14), channel_id=1, source_target_pairs={{8,0},{9,1},{10,2},{11,3},{12,4},{13,5},{14,6},{15,7},{16,8},{17,9... | collective-permute-start | bytes 98312 | tf_op jit(solution)/shard_map/ppermute | solution.py:51
  113.9 6.4 %all-to-all-done.2 = bf16[8,32,512]{2,1,0:T(8,128)(2,1)S(1)} async-done(((bf16[8,32,512]{2,1,0:T(8,128)(2,1)}), bf16[8,32,512]{2,1,0:T(8,128)(2,1)S(1)}, u32[]{:S(2)}, u32[]{:S(2)}) %all-to-all-start.2) | async-done | bytes 262176 | tf_op jit(solution)/shard_map/all_to_all | solution.py:121
  120.4 1.7 %fusion.28 = f32[32,512]{1,0:T(8,128)S(1)} fusion(f32[1,512,512]{2,1,0:T(8,128)} %param.11, f32[32,512]{1,0:T(8,128)S(1)} %convert_reduce_fusion, f32[32,512]{1,0:T(8,128)S(1)} %bitcast.99, bf16[32,512]{1,0:T(8,128)(2,1)} %collective-permute-done.9, f32[512]{0:T(512)S(1)} %copy-done.15), kind=kOutput, calls=%fused_computation.30 | convolution fusion | flops 50397184 | bytes 1280000 | tf_op jit(solution)/shard_map/dot_general | solution.py:55
  122.2 1.2 collective-permute-done.10
  123.5 0.4 select_add_fusion.2
  123.9 0.5 collective-permute-start.11
  124.4 3.8 %collective-permute-done.11 = f32[32,512]{1,0:T(8,128)S(1)} collective-permute-done((f32[32,512]{1,0:T(8,128)S(1)}, f32[32,512]{1,0:T(8,128)S(1)}, u32[]{:S(2)}, u32[]{:S(2)}) %collective-permute-start.11) | collective-permute-done | bytes 65568 | tf_op jit(solution)/shard_map/ppermute | solution.py:51
  128.7 0.7 collective-permute-start.12
  129.4 0.4 convolution_add_fusion.1
  129.8 0.8 collective-permute-start.13
  130.6 0.4 convolution_add_fusion
  131.1 1.4 collective-permute-start.14
  132.5 8.5 %collective-permute-done.14 = f32[32,512]{1,0:T(8,128)S(1)} collective-permute-done((f32[32,512]{1,0:T(8,128)S(1)}, f32[32,512]{1,0:T(8,128)S(1)}, u32[]{:S(2)}, u32[]{:S(2)}) %collective-permute-start.14) | collective-permute-done | bytes 65568 | tf_op jit(solution)/shard_map/ppermute | solution.py:51
  141.5 0.4 fusion.56
  141.9 0.4 select_add_fusion
  142.4 15.6 %all_to_all.22 = f32[8,32,512]{2,1,0:T(8,128)S(1)} all-to-all(f32[8,32,512]{2,1,0:T(8,128)S(1)} %broadcast_in_dim.22), channel_id=1, replica_groups=mesh['chain_0'=4,'chain_1'=2,'chain_2'=2,'tech'=4,'blk'=2] {'tech','blk'}, dimensions={0} | all-to-all | bytes 1048576 | tf_op jit(solution)/shard_map/all_to_all | solution.py:67
  158.0 1.0 copy.14
  (72 shorter events, 4.6 us)
Async XLA Ops:
  0.6 34.4 %copy-start = (bf16[1,1,1536,512]{3,2,1,0:T(8,128)(2,1)S(1)}, bf16[1,1,1536,512]{3,2,1,0:T(8,128)(2,1)}, u32[]{:S(2)}) copy-start(bf16[1,1,1536,512]{3,2,1,0:T(8,128)(2,1)} %param.8) | copy-start | bytes 4718596
  0.6 4.9 %copy-start.3 = (f32[1,512,512]{2,1,0:T(8,128)S(1)}, f32[1,512,512]{2,1,0:T(8,128)}, u32[]{:S(2)}) copy-start(f32[1,512,512]{2,1,0:T(8,128)} %param.11) | copy-start | bytes 3145732
  0.7 4.9 %copy-start.15 = (f32[512]{0:T(512)S(1)}, f32[512]{0:T(512)}, u32[]{:S(2)}) copy-start(f32[512]{0:T(512)} %param.12) | copy-start | bytes 6148
  0.7 6.0 %copy-start.16 = (s32[1,1,512]{2,1,0:T(1,128)S(1)}, s32[1,1,512]{2,1,0:T(1,128)}, u32[]{:S(2)}) copy-start(s32[1,1,512]{2,1,0:T(1,128)} %param.10) | copy-start | bytes 6148
  2.2 9.4 %copy-start.11 = (bf16[1,1,1536,256]{2,3,1,0:T(8,128)(2,1)}, bf16[1,1,1536,256]{2,3,1,0:T(8,128)(2,1)S(1)}, u32[]{:S(2)}) copy-start(bf16[1,1,1536,256]{2,3,1,0:T(8,128)(2,1)S(1)} %copy.12) | copy-start | bytes 2359300
  2.2 21.0 %collective-permute-start = (bf16[1536,256]{0,1:T(8,128)(2,1)S(1)}, bf16[1536,256]{0,1:T(8,128)(2,1)}, u32[]{:S(2)}, u32[]{:S(2)}) collective-permute-start(bf16[1536,256]{0,1:T(8,128)(2,1)S(1)} %bitcast.92), channel_id=1, source_target_pairs={{0,1},{1,0},{2,3},{3,2},{4,5},{5,4},{6,7},{7,6},{8,9},{9,8},{10,11... | collective-permute-start | bytes 2359304 | tf_op jit(solution)/shard_map/ppermute | solution.py:51
  6.6 24.2 %collective-permute-start.1 = (f32[512,512]{1,0:T(8,128)}, f32[512,512]{1,0:T(8,128)}, u32[]{:S(2)}, u32[]{:S(2)}) collective-permute-start(f32[512,512]{1,0:T(8,128)} %bitcast_multiply_fusion), channel_id=1, source_target_pairs={{0,8},{1,9},{2,10},{3,11},{4,12},{5,13},{6,14},{7,15},{8,0},{9,1},... | collective-permute-start | bytes 3145736 | tf_op jit(solution)/shard_map/ppermute | solution.py:51
  32.2 21.1 %copy-start.7 = (f32[512,512]{1,0:T(8,128)}, f32[512,512]{1,0:T(8,128)S(1)}, u32[]{:S(2)}) copy-start(f32[512,512]{1,0:T(8,128)S(1)} %get-tuple-element.17) | copy-start | bytes 3145732
  32.3 41.7 %copy-start.5 = (f32[512,512]{1,0:T(8,128)}, f32[512,512]{1,0:T(8,128)S(1)}, u32[]{:S(2)}) copy-start(f32[512,512]{1,0:T(8,128)S(1)} %get-tuple-element.18) | copy-start | bytes 3145732
  33.3 40.2 %copy-start.9 = (f32[512,512]{1,0:T(8,128)}, f32[512,512]{1,0:T(8,128)S(1)}, u32[]{:S(2)}) copy-start(f32[512,512]{1,0:T(8,128)S(1)} %get-tuple-element.21) | copy-start | bytes 3145732
  33.4 18.2 %copy-start.4 = (f32[1,512,512]{2,1,0:T(8,128)S(1)}, f32[1,512,512]{2,1,0:T(8,128)}, u32[]{:S(2)}) copy-start(f32[1,512,512]{2,1,0:T(8,128)} %param.11) | copy-start | bytes 3145732
  33.4 18.2 %collective-permute-start.2 = (bf16[512,512]{1,0:T(8,128)(2,1)S(1)}, bf16[512,512]{1,0:T(8,128)(2,1)S(1)}, u32[]{:S(2)}, u32[]{:S(2)}) collective-permute-start(bf16[512,512]{1,0:T(8,128)(2,1)S(1)} %get-tuple-element.26), channel_id=1, source_target_pairs={{0,16},{1,17},{2,18},{3,19},{4,20},{5,21},{6,22},{7,23},{8,24},{9,... | collective-permute-start | bytes 1572872 | tf_op jit(solution)/shard_map/ppermute | solution.py:51
  52.0 1.3 collective-permute-start.3
  52.1 52.4 %slice-start = ((s8[9437184]{0:T(1024)(128)(4,1)}), s8[4194304]{0:T(1024)(128)(4,1)S(1)}, s32[]{:S(2)}) async-start(s8[9437184]{0:T(1024)(128)(4,1)} %bitcast.101), calls=%async_computation.4 | async-start | bytes 8388608
  53.1 7.2 %copy-start.1 = (f32[512,512]{1,0:T(8,128)}, f32[512,512]{1,0:T(8,128)S(1)}, u32[]{:S(2)}) copy-start(f32[512,512]{1,0:T(8,128)S(1)} %fusion.34) | copy-start | bytes 3145732
  53.7 4.4 %collective-permute-start.4 = (f32[32,512]{1,0:T(8,128)S(1)}, f32[32,512]{1,0:T(8,128)S(1)}, u32[]{:S(2)}, u32[]{:S(2)}) collective-permute-start(f32[32,512]{1,0:T(8,128)S(1)} %select_add_fusion.4), channel_id=1, source_target_pairs={{0,16},{1,17},{2,18},{3,19},{4,20},{5,21},{6,22},{7,23},{8,24},{9,... | collective-permute-start | bytes 196616 | tf_op jit(solution)/shard_map/ppermute | solution.py:51
  54.4 50.1 %slice-start.1 = ((s8[9437184]{0:T(1024)(128)(4,1)}), s8[4194304]{0:T(1024)(128)(4,1)S(1)}, s32[]{:S(2)}) async-start(s8[9437184]{0:T(1024)(128)(4,1)} %bitcast.101), calls=%async_computation.5 | async-start | bytes 8388608
  58.6 0.7 collective-permute-start.5
  59.7 0.7 collective-permute-start.6
  60.8 12.3 %collective-permute-start.7 = (f32[32,512]{1,0:T(8,128)S(1)}, f32[32,512]{1,0:T(8,128)S(1)}, u32[]{:S(2)}, u32[]{:S(2)}) collective-permute-start(f32[32,512]{1,0:T(8,128)S(1)} %convolution_add_fusion.3), channel_id=1, source_target_pairs={{64,96},{65,97},{66,98},{67,99},{68,100},{69,101},{70,102},{71,103... | collective-permute-start | bytes 196616 | tf_op jit(solution)/shard_map/ppermute | solution.py:51
  74.0 13.4 %copy-start.12 = (bf16[1,1,1536,256]{2,3,1,0:T(8,128)(2,1)S(1)}, bf16[1,1,1536,256]{2,3,1,0:T(8,128)(2,1)}, u32[]{:S(2)}) copy-start(bf16[1,1,1536,256]{2,3,1,0:T(8,128)(2,1)} %copy-done.11) | copy-start | bytes 2359300
  74.4 12.8 %copy-start.14 = (bf16[32,512]{1,0:T(8,128)(2,1)}, bf16[32,512]{1,0:T(8,128)(2,1)S(1)}, u32[]{:S(2)}) copy-start(bf16[32,512]{1,0:T(8,128)(2,1)S(1)} %add_convert_fusion) | copy-start | bytes 98308
  74.4 30.1 %slice-start.2 = ((s8[9437184]{0:T(1024)(128)(4,1)}), s8[1048576]{0:T(1024)(128)(4,1)S(1)}, s32[]{:S(2)}) async-start(s8[9437184]{0:T(1024)(128)(4,1)} %bitcast.101), calls=%async_computation.6 | async-start | bytes 2097152
  88.1 16.4 %collective-permute-start.8 = (bf16[1536,256]{0,1:T(8,128)(2,1)S(1)}, bf16[1536,256]{0,1:T(8,128)(2,1)S(1)}, u32[]{:S(2)}, u32[]{:S(2)}) collective-permute-start(bf16[1536,256]{0,1:T(8,128)(2,1)S(1)} %get-tuple-element.32), channel_id=1, source_target_pairs={{0,1},{1,0},{2,3},{3,2},{4,5},{5,4},{6,7},{7,6},{8,9},{9,8},{10,11... | collective-permute-start | bytes 2359304 | tf_op jit(solution)/shard_map/ppermute | solution.py:51
  107.2 1.3 copy-start.13
  108.5 11.8 %all-to-all-start.2 = ((bf16[8,32,512]{2,1,0:T(8,128)(2,1)}), bf16[8,32,512]{2,1,0:T(8,128)(2,1)S(1)}, u32[]{:S(2)}, u32[]{:S(2)}) async-start(bf16[8,32,512]{2,1,0:T(8,128)(2,1)} %bitcast.97), calls=%async_computation.2 | async-start | bytes 524288 | tf_op jit(solution)/shard_map/all_to_all | solution.py:121
  112.0 8.4 %collective-permute-start.9 = (bf16[32,512]{1,0:T(8,128)(2,1)}, bf16[32,512]{1,0:T(8,128)(2,1)}, u32[]{:S(2)}, u32[]{:S(2)}) collective-permute-start(bf16[32,512]{1,0:T(8,128)(2,1)} %copy-done.14), channel_id=1, source_target_pairs={{8,0},{9,1},{10,2},{11,3},{12,4},{13,5},{14,6},{15,7},{16,8},{17,9... | collective-permute-start | bytes 98312 | tf_op jit(solution)/shard_map/ppermute | solution.py:51
  120.3 3.1 %copy-start.8 = (f32[512,512]{1,0:T(8,128)S(1)}, f32[512,512]{1,0:T(8,128)}, u32[]{:S(2)}) copy-start(f32[512,512]{1,0:T(8,128)} %copy-done.7) | copy-start | bytes 3145732
  122.1 7.2 %copy-start.2 = (f32[512,512]{1,0:T(8,128)S(1)}, f32[512,512]{1,0:T(8,128)}, u32[]{:S(2)}) copy-start(f32[512,512]{1,0:T(8,128)} %copy-done.1) | copy-start | bytes 3145732
  122.1 1.3 collective-permute-start.10
  123.9 4.3 %collective-permute-start.11 = (f32[32,512]{1,0:T(8,128)S(1)}, f32[32,512]{1,0:T(8,128)S(1)}, u32[]{:S(2)}, u32[]{:S(2)}) collective-permute-start(f32[32,512]{1,0:T(8,128)S(1)} %select_add_fusion.2), channel_id=1, source_target_pairs={{0,16},{1,17},{2,18},{3,19},{4,20},{5,21},{6,22},{7,23},{8,24},{9,... | collective-permute-start | bytes 196616 | tf_op jit(solution)/shard_map/ppermute | solution.py:51
  128.7 0.7 collective-permute-start.12
  129.8 11.7 %copy-start.10 = (f32[512,512]{1,0:T(8,128)S(1)}, f32[512,512]{1,0:T(8,128)}, u32[]{:S(2)}) copy-start(f32[512,512]{1,0:T(8,128)} %copy-done.9) | copy-start | bytes 3145732
  129.8 0.8 collective-permute-start.13
  131.1 10.8 %copy-start.6 = (f32[512,512]{1,0:T(8,128)S(1)}, f32[512,512]{1,0:T(8,128)}, u32[]{:S(2)}) copy-start(f32[512,512]{1,0:T(8,128)} %copy-done.5) | copy-start | bytes 3145732
  131.1 9.9 %collective-permute-start.14 = (f32[32,512]{1,0:T(8,128)S(1)}, f32[32,512]{1,0:T(8,128)S(1)}, u32[]{:S(2)}, u32[]{:S(2)}) collective-permute-start(f32[32,512]{1,0:T(8,128)S(1)} %convolution_add_fusion), channel_id=1, source_target_pairs={{64,96},{65,97},{66,98},{67,99},{68,100},{69,101},{70,102},{71,103... | collective-permute-start | bytes 196616 | tf_op jit(solution)/shard_map/ppermute | solution.py:51
where the time goes:
time: 160 us; the launch traced here: 159 us
  waiting for transfers between devices  61.4 us (38%)
  blocking collectives  44.2 us (28%)
  matrix products  22.1 us (14%)
  starting transfers between devices  18.2 us (11%)
  local copies, waits for them, and re-layouts  9.28 us (6%)
  other arithmetic  2.64 us (2%)
    ppermute x15, waiting for transfers between devices, moved(): return lax.ppermute(value, AXES, pairs)  54.9 us
    all_to_all x2, blocking collectives, collected(): lax.all_to_all(copies, REPLICAS, split_axis=0, concat_axis=0, tiled=True)  28.4 us
    all_to_all x1, blocking collectives, summed(): lax.all_to_all(terms.reshape(8, samples, terms.shape[1]), REPLICAS, split...  15.9 us
    ppermute x15, starting transfers between devices, moved(): return lax.ppermute(value, AXES, pairs)  14.8 us
    dot_general x19, matrix products, exact(): return jnp.dot(left, right, precision=lax.Precision.HIGH)  10.5 us
    dot_general x2, matrix products, solved(): jnp.dot(inverse_rows, residual, preferred_element_type=jnp.float32)  9.02 us
    all_to_all x1, waiting for transfers between devices, summed(): lax.all_to_all(terms.reshape(8, samples, terms.shape[1]), REPLICAS, split...  6.44 us
    all_to_all x1, starting transfers between devices, summed(): lax.all_to_all(terms.reshape(8, samples, terms.shape[1]), REPLICAS, split...  3.41 us
  transfers between devices with their start and end apart: 16, of which 9 were waited for; matrix products, arithmetic and copies ran while one was open for 10% of the time, Pallas kernels for 0%

commit v1 on v0

--- a/solution.py
+++ b/solution.py
@@ -53,13 +53,6 @@
 
 def exact(left, right):
     return jnp.dot(left, right, precision=lax.Precision.HIGH)
-
-
-def both_halves(own, other, which):
-    rows = own.shape[0]
-    whole = jnp.zeros((2 * rows, *own.shape[1:]), own.dtype)
-    whole = lax.dynamic_update_slice_in_dim(whole, own, which * rows, 0)
-    return lax.dynamic_update_slice_in_dim(whole, other, (1 - which) * rows, 0)
 
 
 def collected(part):
@@ -104,10 +97,13 @@
     own_map = jnp.where(early_core, step_first, pair)
     pair_other = moved(pair.astype(jnp.bfloat16), CHIP_SWAP)
 
-    def solved(residual):
-        return row_major(
-            seen_rows * jnp.dot(inverse_rows, residual, preferred_element_type=jnp.float32)
-        )
+    def added(columns, rows):
+        product = jnp.dot(columns, rows, preferred_element_type=jnp.float32)
+        return lax.optimization_barrier(product)
+
+    def solved(part, columns, rows):
+        product = jnp.dot(columns, rows, preferred_element_type=jnp.float32)
+        return row_major(seen_rows * (part + product))
 
     def terms_of(coords):
         return lax.dot_general(
@@ -133,7 +129,12 @@
         )
         return (rhs.astype(jnp.float32) - product).astype(jnp.bfloat16)
 
-    coords = solved(both_halves(rhs_rows, rhs_other, half))
+    width = inverse_rows.shape[0]
+    columns_own = lax.dynamic_slice_in_dim(inverse_rows, half * width, width, 1)
+    columns_other = lax.dynamic_slice_in_dim(inverse_rows, (1 - half) * width, width, 1)
+    columns_own, columns_other = lax.optimization_barrier((columns_own, columns_other))
+    part = added(columns_own, rhs_rows)
+    coords = solved(part, columns_other, rhs_other)
     terms = terms_of(lax.optimization_barrier(coords))
     terms, week_rhs, pair, own_map, step_first, step_second, early_core, early_chip = (
         lax.optimization_barrier(
@@ -154,7 +155,7 @@
         first = jnp.where(early_core, offset, offset_other)
         second = jnp.where(early_core, offset_other, offset)
         chip_end = second + exact(first, step_second)
-        chip_other = moved(chip_end, CHIP_SWAP)
+        chip_other = moved(chip_end.astype(jnp.bfloat16), CHIP_SWAP).astype(jnp.float32)
         chip_first = jnp.where(early_chip, chip_end, chip_other)
         chip_second = jnp.where(early_chip, chip_other, chip_end)
         group_end = chip_second + exact(chip_first, pair_second)
@@ -165,7 +166,9 @@
         )
         carried = jnp.zeros_like(offset)
         for hop in Z_HOPS:
-            carried = carried + moved(group_end + exact(carried, group), hop)
+            leaving = group_end + exact(carried, group)
+            arrived = moved(leaving.astype(jnp.bfloat16), hop)
+            carried = carried + arrived.astype(jnp.float32)
         entering = jnp.where(early_chip, carried, exact(carried, pair_first))
         return inside + exact(entering, own_map)
 
@@ -176,12 +179,13 @@
     shared_low = shared.astype(jnp.bfloat16)
     shared_all = collected(shared_low)
     later = moved(shared_low, LATER).astype(jnp.float32)
-    residual_own = left(rhs_rows, coupling_rows, shared_all)
+    residual_own = row_major(left(rhs_rows, coupling_rows, shared_all))
     residual_other = moved(residual_own, BLK_SWAP)
-    coords = solved(both_halves(residual_own, residual_other, half))
+    part = added(columns_own, residual_own)
+    coords = solved(part, columns_other, residual_other)
     station_sum = summed(terms_of(coords))
     shared = chain(exact(week_rhs + weight * later - station_sum, inverse), maps)
-    result = collected(shared).T
+    result = collected(shared.astype(jnp.bfloat16)).T.astype(jnp.float32)
     return (coords[None, None], result[None])
 
 

time: 160 us -> 147 us (0.919)
  waiting for transfers between devices: 61.4 us -> 48.4 us
  blocking collectives: 44.2 us -> 42 us
    ppermute x15, waiting for transfers between devices: 54.9 us -> 42 us  [moved(): return lax.ppermute(value, AXES, pairs)]
    dynamic_slice x0 -> x1, local copies, waits for them, and re-layouts: none -> 8.03 us  [layer(): lax.dynamic_slice_in_dim(inverse_rows, (1 - half) * width, width, 1)]
    all_to_all x2, blocking collectives: 28.4 us -> 26.1 us  [collected(): lax.all_to_all(copies, REPLICAS, split_axis=0, concat_axis=0, tiled=True)]
    another operation x4 -> x2, local copies, waits for them, and re-layouts: 3.19 us -> 1.18 us
    dot_general x2 -> x4, matrix products: 9.02 us -> 9.55 us  [the longest x2 5.54 us: added(): product = jnp.dot(columns, rows, preferred_element_type=jnp.float32)]
  transfers between devices with their start and end apart: 16 -> 16, of which waited for: 9 -> 9; matrix products, arithmetic and copies ran while one was open for 10% -> 14% of each run, Pallas kernels for 0% -> 0%
where the time goes in v1:
time: 147 us; the launch traced here: 146 us
  waiting for transfers between devices  48.4 us (33%)
  blocking collectives  42 us (29%)
  matrix products  22.4 us (15%)
  starting transfers between devices  18.4 us (13%)
  local copies, waits for them, and re-layouts  10.7 us (7%)
  other arithmetic  2.94 us (2%)
    ppermute x15, waiting for transfers between devices, moved(): return lax.ppermute(value, AXES, pairs)  42 us
    all_to_all x2, blocking collectives, collected(): lax.all_to_all(copies, REPLICAS, split_axis=0, concat_axis=0, tiled=True)  26.1 us
    all_to_all x1, blocking collectives, summed(): lax.all_to_all(terms.reshape(8, samples, terms.shape[1]), REPLICAS, split...  15.9 us
    ppermute x15, starting transfers between devices, moved(): return lax.ppermute(value, AXES, pairs)  14.9 us
    dot_general x19, matrix products, exact(): return jnp.dot(left, right, precision=lax.Precision.HIGH)  10.4 us
    dynamic_slice x1, local copies, waits for them, and re-layouts, layer(): lax.dynamic_slice_in_dim(inverse_rows, (1 - half) * width, width, 1)  8.03 us
    all_to_all x1, waiting for transfers between devices, summed(): lax.all_to_all(terms.reshape(8, samples, terms.shape[1]), REPLICAS, split...  6.44 us
    dot_general x2, matrix products, added(): product = jnp.dot(columns, rows, preferred_element_type=jnp.float32)  5.54 us
  transfers between devices with their start and end apart: 16, of which 9 were waited for; matrix products, arithmetic and copies ran while one was open for 14% of the time, Pallas kernels for 0%

profile of v1, /device:TPU:96, one launch (start us, length us, event | category | flops | bytes accessed | tf_op | source)
XLA Modules:
  0.0 146.1 jit_solution(14696751831863931564)
XLA Ops:
  0.6 3.3 %collective-permute-start = (bf16[1536,256]{1,0:T(8,128)(2,1)}, bf16[1536,256]{1,0:T(8,128)(2,1)}, u32[]{:S(2)}, u32[]{:S(2)}) collective-permute-start(bf16[1536,256]{1,0:T(8,128)(2,1)} %bitcast.84), channel_id=1, source_target_pairs={{0,1},{1,0},{2,3},{3,2},{4,5},{5,4},{6,7},{7,6},{8,9},{9,8},{10,11... | collective-permute-start | bytes 2359304 | tf_op jit(solution)/shard_map/ppermute | solution.py:51
  3.9 1.4 bitcast_multiply_fusion
  5.4 8.0 %dynamic-slice_bitcast_fusion = (bf16[1536,1536]{1,0:T(8,128)(2,1)}, bf16[1536,1536]{1,0:T(8,128)(2,1)}) fusion(bf16[1,1,1536,3072]{3,2,1,0:T(8,128)(2,1)} %param.7, s32[]{:T(128)S(6)} %select_n.106, s32[]{:T(128)S(6)} %select_n.105), kind=kLoop, calls=%fused_computation | loop fusion | bytes 18874376 | tf_op jit(solution)/shard_map/dynamic_slice | solution.py:134
  13.8 1.1 constant_dynamic-slice_fusion
  15.0 4.1 %fusion.44 = f32[1536,256]{1,0:T(8,128)S(1)} fusion(bf16[1536,1536]{1,0:T(8,128)(2,1)} %get-tuple-element.14, bf16[1,1,1536,256]{3,2,1,0:T(8,128)(2,1)} %param.9), kind=kOutput, calls=%fused_computation.77 | convolution fusion | flops 1207959552 | bytes 7077888 | tf_op jit(solution)/shard_map/dot_general | solution.py:101
  19.1 2.7 %collective-permute-done = bf16[1536,256]{1,0:T(8,128)(2,1)} collective-permute-done((bf16[1536,256]{1,0:T(8,128)(2,1)}, bf16[1536,256]{1,0:T(8,128)(2,1)}, u32[]{:S(2)}, u32[]{:S(2)}) %collective-permute-start) | collective-permute-done | bytes 786464 | tf_op jit(solution)/shard_map/ppermute | solution.py:51
  21.8 2.6 %fusion.2 = bf16[1536,256]{1,0:T(8,128)(2,1)S(1)} fusion(f32[1536,256]{1,0:T(8,128)S(1)} %fusion.44, bf16[1536,1536]{1,0:T(8,128)(2,1)S(1)} %bitcast.75, bf16[1536,256]{1,0:T(8,128)(2,1)} %collective-permute-done, f32[1536]{0:T(1024)S(1)} %convert_element_type.111), kind=kOutput, calls=%fused_computation.7 | convolution fusion | flops 1209139200 | bytes 7870464 | tf_op jit(solution)/shard_map/dot_general | solution.py:105
  24.4 1.4 broadcast_select_fusion.1
  25.9 1.1 fusion.49
  27.0 1.7 %collective-permute-start.2 = (bf16[512,512]{1,0:T(8,128)(2,1)S(1)}, bf16[512,512]{1,0:T(8,128)(2,1)S(1)}, u32[]{:S(2)}, u32[]{:S(2)}) collective-permute-start(bf16[512,512]{1,0:T(8,128)(2,1)S(1)} %get-tuple-element.32), channel_id=1, source_target_pairs={{0,16},{1,17},{2,18},{3,19},{4,20},{5,21},{6,22},{7,23},{8,24},{9,... | collective-permute-start | bytes 1572872 | tf_op jit(solution)/shard_map/ppermute | solution.py:51
  28.6 0.6 fusion.9
  29.2 15.9 %all_to_all.20 = bf16[8,32,512]{2,1,0:T(8,128)(2,1)S(1)} all-to-all(bf16[8,32,512]{2,1,0:T(8,128)(2,1)S(1)} %bitcast.81), channel_id=1, replica_groups=mesh['chain_0'=4,'chain_1'=2,'chain_2'=2,'tech'=4,'blk'=2] {'tech','blk'}, dimensions={0} | all-to-all | bytes 524288 | tf_op jit(solution)/shard_map/all_to_all | solution.py:117
  45.2 0.4 fusion.23
  45.7 1.0 fusion.28
  47.0 0.4 fusion.50
  48.0 3.4 %collective-permute-done.4 = bf16[32,512]{1,0:T(8,128)(2,1)S(1)} collective-permute-done((bf16[32,512]{1,0:T(8,128)(2,1)S(1)}, bf16[32,512]{1,0:T(8,128)(2,1)S(1)}, u32[]{:S(2)}, u32[]{:S(2)}) %collective-permute-start.4) | collective-permute-done | bytes 32800 | tf_op jit(solution)/shard_map/ppermute | solution.py:51
  51.4 0.4 add_convert_fusion.3
  51.8 0.7 collective-permute-start.5
  52.8 0.7 collective-permute-start.6
  53.9 1.4 collective-permute-start.7
  55.4 10.0 %collective-permute-done.7 = bf16[32,512]{1,0:T(8,128)(2,1)S(1)} collective-permute-done((bf16[32,512]{1,0:T(8,128)(2,1)S(1)}, bf16[32,512]{1,0:T(8,128)(2,1)S(1)}, u32[]{:S(2)}, u32[]{:S(2)}) %collective-permute-start.7) | collective-permute-done | bytes 32800 | tf_op jit(solution)/shard_map/ppermute | solution.py:51
  66.2 0.4 add_convert_fusion.2
  66.7 12.6 %all_to_all.21 = bf16[8,32,512]{2,1,0:T(8,128)(2,1)S(1)} all-to-all(bf16[8,32,512]{2,1,0:T(8,128)(2,1)S(1)} %broadcast_in_dim.23), channel_id=1, replica_groups=mesh['chain_0'=4,'chain_1'=2,'chain_2'=2,'tech'=4,'blk'=2] {'tech','blk'}, dimensions={0} | all-to-all | bytes 524288 | tf_op jit(solution)/shard_map/all_to_all | solution.py:60
  79.3 0.6 fusion.3
  80.0 1.5 collective-permute-start.8
  81.4 1.4 fusion.53
  82.9 13.3 %collective-permute-done.8 = bf16[1536,256]{1,0:T(8,128)(2,1)S(1)} collective-permute-done((bf16[1536,256]{1,0:T(8,128)(2,1)S(1)}, bf16[1536,256]{1,0:T(8,128)(2,1)S(1)}, u32[]{:S(2)}, u32[]{:S(2)}) %collective-permute-start.8) | collective-permute-done | bytes 786464 | tf_op jit(solution)/shard_map/ppermute | solution.py:51
  96.2 1.4 fusion.1
  97.6 1.3 fusion.12
  99.0 3.4 %all-to-all-start.2 = ((bf16[8,32,512]{2,1,0:T(8,128)(2,1)}), bf16[8,32,512]{2,1,0:T(8,128)(2,1)S(1)}, u32[]{:S(2)}, u32[]{:S(2)}) async-start(bf16[8,32,512]{2,1,0:T(8,128)(2,1)} %bitcast.82), calls=%async_computation.2 | async-start | bytes 524288 | tf_op jit(solution)/shard_map/all_to_all | solution.py:117
  102.4 1.9 %collective-permute-start.9 = (bf16[32,512]{1,0:T(8,128)(2,1)}, bf16[32,512]{1,0:T(8,128)(2,1)}, u32[]{:S(2)}, u32[]{:S(2)}) collective-permute-start(bf16[32,512]{1,0:T(8,128)(2,1)} %copy-done.12), channel_id=1, source_target_pairs={{8,0},{9,1},{10,2},{11,3},{12,4},{13,5},{14,6},{15,7},{16,8},{17,9... | collective-permute-start | bytes 98312 | tf_op jit(solution)/shard_map/ppermute | solution.py:51
  104.3 6.4 %all-to-all-done.2 = bf16[8,32,512]{2,1,0:T(8,128)(2,1)S(1)} async-done(((bf16[8,32,512]{2,1,0:T(8,128)(2,1)}), bf16[8,32,512]{2,1,0:T(8,128)(2,1)S(1)}, u32[]{:S(2)}, u32[]{:S(2)}) %all-to-all-start.2) | async-done | bytes 262176 | tf_op jit(solution)/shard_map/all_to_all | solution.py:117
  110.8 1.7 %fusion.21 = f32[32,512]{1,0:T(8,128)S(1)} fusion(f32[1,512,512]{2,1,0:T(8,128)} %param.11, f32[32,512]{1,0:T(8,128)S(1)} %convert_reduce_fusion, f32[32,512]{1,0:T(8,128)S(1)} %bitcast.86, bf16[32,512]{1,0:T(8,128)(2,1)} %collective-permute-done.9, f32[512]{0:T(512)S(1)} %copy-done.13), kind=kOutput, calls=%fused_computation.32 | convolution fusion | flops 50397184 | bytes 1280000 | tf_op jit(solution)/shard_map/dot_general | solution.py:55
  112.6 1.2 collective-permute-done.10
  113.9 0.4 fusion.51
  114.3 0.5 collective-permute-start.11
  114.9 3.5 %collective-permute-done.11 = bf16[32,512]{1,0:T(8,128)(2,1)S(1)} collective-permute-done((bf16[32,512]{1,0:T(8,128)(2,1)S(1)}, bf16[32,512]{1,0:T(8,128)(2,1)S(1)}, u32[]{:S(2)}, u32[]{:S(2)}) %collective-permute-start.11) | collective-permute-done | bytes 32800 | tf_op jit(solution)/shard_map/ppermute | solution.py:51
  118.3 0.4 add_convert_fusion.1
  118.8 0.7 collective-permute-start.12
  119.8 0.8 collective-permute-start.13
  120.6 0.4 fusion.20
  121.0 1.4 collective-permute-start.14
  122.5 7.7 %collective-permute-done.14 = bf16[32,512]{1,0:T(8,128)(2,1)S(1)} collective-permute-done((bf16[32,512]{1,0:T(8,128)(2,1)S(1)}, bf16[32,512]{1,0:T(8,128)(2,1)S(1)}, u32[]{:S(2)}, u32[]{:S(2)}) %collective-permute-start.14) | collective-permute-done | bytes 32800 | tf_op jit(solution)/shard_map/ppermute | solution.py:51
  130.2 0.4 convolution_select_fusion
  130.6 0.4 fusion.54
  131.1 0.4 add_convert_fusion
  131.5 13.5 %all_to_all.22 = bf16[8,32,512]{2,1,0:T(8,128)(2,1)S(1)} all-to-all(bf16[8,32,512]{2,1,0:T(8,128)(2,1)S(1)} %broadcast_in_dim.25), channel_id=1, replica_groups=mesh['chain_0'=4,'chain_1'=2,'chain_2'=2,'tech'=4,'blk'=2] {'tech','blk'}, dimensions={0} | all-to-all | bytes 524288 | tf_op jit(solution)/shard_map/all_to_all | solution.py:60
  145.1 1.0 copy.12
  (72 shorter events, 3.7 us)
Async XLA Ops:
  0.6 28.0 %copy-start = (bf16[1,1,1536,512]{3,2,1,0:T(8,128)(2,1)S(1)}, bf16[1,1,1536,512]{3,2,1,0:T(8,128)(2,1)}, u32[]{:S(2)}) copy-start(bf16[1,1,1536,512]{3,2,1,0:T(8,128)(2,1)} %param.8) | copy-start | bytes 4718596
  0.6 21.2 %collective-permute-start = (bf16[1536,256]{1,0:T(8,128)(2,1)}, bf16[1536,256]{1,0:T(8,128)(2,1)}, u32[]{:S(2)}, u32[]{:S(2)}) collective-permute-start(bf16[1536,256]{1,0:T(8,128)(2,1)} %bitcast.84), channel_id=1, source_target_pairs={{0,1},{1,0},{2,3},{3,2},{4,5},{5,4},{6,7},{7,6},{8,9},{9,8},{10,11... | collective-permute-start | bytes 2359304 | tf_op jit(solution)/shard_map/ppermute | solution.py:51
  5.3 19.1 %collective-permute-start.1 = (f32[512,512]{1,0:T(8,128)S(1)}, f32[512,512]{1,0:T(8,128)}, u32[]{:S(2)}, u32[]{:S(2)}) collective-permute-start(f32[512,512]{1,0:T(8,128)S(1)} %bitcast_multiply_fusion), channel_id=1, source_target_pairs={{0,8},{1,9},{2,10},{3,11},{4,12},{5,13},{6,14},{7,15},{8,0},{9,1},... | collective-permute-start | bytes 3145736 | tf_op jit(solution)/shard_map/ppermute | solution.py:51
  5.4 8.0 %copy-start.14 = (s32[1,1,512]{2,1,0:T(1,128)S(1)}, s32[1,1,512]{2,1,0:T(1,128)}, u32[]{:S(2)}) copy-start(s32[1,1,512]{2,1,0:T(1,128)} %param.10) | copy-start | bytes 6148
  14.9 7.0 %slice-start = ((s8[4718592]{0:T(1024)(128)(4,1)}), s8[524288]{0:T(1024)(128)(4,1)S(1)}, s32[]{:S(2)}) async-start(s8[4718592]{0:T(1024)(128)(4,1)} %bitcast.74), calls=%async_computation.4 | async-start | bytes 1048576
  15.0 6.9 %slice-start.1 = ((s8[4718592]{0:T(1024)(128)(4,1)}), s8[4194304]{0:T(1024)(128)(4,1)S(1)}, s32[]{:S(2)}) async-start(s8[4718592]{0:T(1024)(128)(4,1)} %bitcast.74), calls=%async_computation.5 | async-start | bytes 8388608
  19.1 5.3 %copy-start.3 = (f32[1,512,512]{2,1,0:T(8,128)S(1)}, f32[1,512,512]{2,1,0:T(8,128)}, u32[]{:S(2)}) copy-start(f32[1,512,512]{2,1,0:T(8,128)} %param.11) | copy-start | bytes 3145732
  19.1 5.3 %copy-start.13 = (f32[512]{0:T(512)S(1)}, f32[512]{0:T(512)}, u32[]{:S(2)}) copy-start(f32[512]{0:T(512)} %param.12) | copy-start | bytes 6148
  25.9 21.1 %copy-start.6 = (f32[512,512]{1,0:T(8,128)}, f32[512,512]{1,0:T(8,128)S(1)}, u32[]{:S(2)}) copy-start(f32[512,512]{1,0:T(8,128)S(1)} %get-tuple-element.21) | copy-start | bytes 3145732
  25.9 40.3 %copy-start.4 = (f32[512,512]{1,0:T(8,128)}, f32[512,512]{1,0:T(8,128)S(1)}, u32[]{:S(2)}) copy-start(f32[512,512]{1,0:T(8,128)S(1)} %get-tuple-element.22) | copy-start | bytes 3145732
  27.0 38.8 %copy-start.8 = (f32[512,512]{1,0:T(8,128)}, f32[512,512]{1,0:T(8,128)S(1)}, u32[]{:S(2)}) copy-start(f32[512,512]{1,0:T(8,128)S(1)} %get-tuple-element.25) | copy-start | bytes 3145732
  27.0 18.2 %collective-permute-start.2 = (bf16[512,512]{1,0:T(8,128)(2,1)S(1)}, bf16[512,512]{1,0:T(8,128)(2,1)S(1)}, u32[]{:S(2)}, u32[]{:S(2)}) collective-permute-start(bf16[512,512]{1,0:T(8,128)(2,1)S(1)} %get-tuple-element.32), channel_id=1, source_target_pairs={{0,16},{1,17},{2,18},{3,19},{4,20},{5,21},{6,22},{7,23},{8,24},{9,... | collective-permute-start | bytes 1572872 | tf_op jit(solution)/shard_map/ppermute | solution.py:51
  45.6 1.3 collective-permute-start.3
  46.7 6.8 %copy-start.1 = (f32[512,512]{1,0:T(8,128)}, f32[512,512]{1,0:T(8,128)S(1)}, u32[]{:S(2)}) copy-start(f32[512,512]{1,0:T(8,128)S(1)} %fusion.28) | copy-start | bytes 3145732
  47.4 4.0 %collective-permute-start.4 = (bf16[32,512]{1,0:T(8,128)(2,1)S(1)}, bf16[32,512]{1,0:T(8,128)(2,1)S(1)}, u32[]{:S(2)}, u32[]{:S(2)}) collective-permute-start(bf16[32,512]{1,0:T(8,128)(2,1)S(1)} %get-tuple-element.35), channel_id=1, source_target_pairs={{0,16},{1,17},{2,18},{3,19},{4,20},{5,21},{6,22},{7,23},{8,24},{9,... | collective-permute-start | bytes 98312 | tf_op jit(solution)/shard_map/ppermute | solution.py:51
  47.6 33.8 %slice-start.4 = ((s8[4718592]{0:T(1024)(128)(4,1)}), s8[4194304]{0:T(1024)(128)(4,1)S(1)}, s32[]{:S(2)}) async-start(s8[4718592]{0:T(1024)(128)(4,1)} %bitcast.78), calls=%async_computation.8 | async-start | bytes 8388608
  51.8 0.7 collective-permute-start.5
  52.8 0.7 collective-permute-start.6
  53.9 27.5 %slice-start.5 = ((s8[4718592]{0:T(1024)(128)(4,1)}), s8[524288]{0:T(1024)(128)(4,1)S(1)}, s32[]{:S(2)}) async-start(s8[4718592]{0:T(1024)(128)(4,1)} %bitcast.78), calls=%async_computation.9 | async-start | bytes 1048576
  53.9 11.4 %collective-permute-start.7 = (bf16[32,512]{1,0:T(8,128)(2,1)S(1)}, bf16[32,512]{1,0:T(8,128)(2,1)S(1)}, u32[]{:S(2)}, u32[]{:S(2)}) collective-permute-start(bf16[32,512]{1,0:T(8,128)(2,1)S(1)} %fusion.18), channel_id=1, source_target_pairs={{64,96},{65,97},{66,98},{67,99},{68,100},{69,101},{70,102},{71,103... | collective-permute-start | bytes 98312 | tf_op jit(solution)/shard_map/ppermute | solution.py:51
  65.8 13.5 %copy-start.11 = (bf16[1,1,1536,256]{3,2,1,0:T(8,128)(2,1)S(1)}, bf16[1,1,1536,256]{3,2,1,0:T(8,128)(2,1)}, u32[]{:S(2)}) copy-start(bf16[1,1,1536,256]{3,2,1,0:T(8,128)(2,1)} %param.9) | copy-start | bytes 2359300
  66.7 13.3 %copy-start.12 = (bf16[32,512]{1,0:T(8,128)(2,1)}, bf16[32,512]{1,0:T(8,128)(2,1)S(1)}, u32[]{:S(2)}) copy-start(bf16[32,512]{1,0:T(8,128)(2,1)S(1)} %add_convert_fusion.2) | copy-start | bytes 98308
  79.3 16.8 %slice-start.2 = ((s8[4718592]{0:T(1024)(128)(4,1)}), s8[4194304]{0:T(1024)(128)(4,1)S(1)}, s32[]{:S(2)}) async-start(s8[4718592]{0:T(1024)(128)(4,1)} %bitcast.76), calls=%async_computation.6 | async-start | bytes 8388608
  80.0 16.2 %slice-start.3 = ((s8[4718592]{0:T(1024)(128)(4,1)}), s8[524288]{0:T(1024)(128)(4,1)S(1)}, s32[]{:S(2)}) async-start(s8[4718592]{0:T(1024)(128)(4,1)} %bitcast.76), calls=%async_computation.7 | async-start | bytes 1048576
  80.0 16.2 %collective-permute-start.8 = (bf16[1536,256]{1,0:T(8,128)(2,1)S(1)}, bf16[1536,256]{1,0:T(8,128)(2,1)S(1)}, u32[]{:S(2)}, u32[]{:S(2)}) collective-permute-start(bf16[1536,256]{1,0:T(8,128)(2,1)S(1)} %fusion.3), channel_id=1, source_target_pairs={{0,1},{1,0},{2,3},{3,2},{4,5},{5,4},{6,7},{7,6},{8,9},{9,8},{10,11... | collective-permute-start | bytes 2359304 | tf_op jit(solution)/shard_map/ppermute | solution.py:51
  97.6 1.3 copy-start.10
  99.0 11.8 %all-to-all-start.2 = ((bf16[8,32,512]{2,1,0:T(8,128)(2,1)}), bf16[8,32,512]{2,1,0:T(8,128)(2,1)S(1)}, u32[]{:S(2)}, u32[]{:S(2)}) async-start(bf16[8,32,512]{2,1,0:T(8,128)(2,1)} %bitcast.82), calls=%async_computation.2 | async-start | bytes 524288 | tf_op jit(solution)/shard_map/all_to_all | solution.py:117
  102.4 8.4 %collective-permute-start.9 = (bf16[32,512]{1,0:T(8,128)(2,1)}, bf16[32,512]{1,0:T(8,128)(2,1)}, u32[]{:S(2)}, u32[]{:S(2)}) collective-permute-start(bf16[32,512]{1,0:T(8,128)(2,1)} %copy-done.12), channel_id=1, source_target_pairs={{8,0},{9,1},{10,2},{11,3},{12,4},{13,5},{14,6},{15,7},{16,8},{17,9... | collective-permute-start | bytes 98312 | tf_op jit(solution)/shard_map/ppermute | solution.py:51
  110.8 3.1 %copy-start.7 = (f32[512,512]{1,0:T(8,128)S(1)}, f32[512,512]{1,0:T(8,128)}, u32[]{:S(2)}) copy-start(f32[512,512]{1,0:T(8,128)} %copy-done.6) | copy-start | bytes 3145732
  112.5 6.9 %copy-start.2 = (f32[512,512]{1,0:T(8,128)S(1)}, f32[512,512]{1,0:T(8,128)}, u32[]{:S(2)}) copy-start(f32[512,512]{1,0:T(8,128)} %copy-done.1) | copy-start | bytes 3145732
  112.5 1.3 collective-permute-start.10
  114.3 4.0 %collective-permute-start.11 = (bf16[32,512]{1,0:T(8,128)(2,1)S(1)}, bf16[32,512]{1,0:T(8,128)(2,1)S(1)}, u32[]{:S(2)}, u32[]{:S(2)}) collective-permute-start(bf16[32,512]{1,0:T(8,128)(2,1)S(1)} %get-tuple-element.39), channel_id=1, source_target_pairs={{0,16},{1,17},{2,18},{3,19},{4,20},{5,21},{6,22},{7,23},{8,24},{9,... | collective-permute-start | bytes 98312 | tf_op jit(solution)/shard_map/ppermute | solution.py:51
  118.8 0.7 collective-permute-start.12
  119.8 10.9 %copy-start.9 = (f32[512,512]{1,0:T(8,128)S(1)}, f32[512,512]{1,0:T(8,128)}, u32[]{:S(2)}) copy-start(f32[512,512]{1,0:T(8,128)} %copy-done.8) | copy-start | bytes 3145732
  119.8 0.8 collective-permute-start.13
  121.0 10.0 %copy-start.5 = (f32[512,512]{1,0:T(8,128)S(1)}, f32[512,512]{1,0:T(8,128)}, u32[]{:S(2)}) copy-start(f32[512,512]{1,0:T(8,128)} %copy-done.4) | copy-start | bytes 3145732
  121.0 9.1 %collective-permute-start.14 = (bf16[32,512]{1,0:T(8,128)(2,1)S(1)}, bf16[32,512]{1,0:T(8,128)(2,1)S(1)}, u32[]{:S(2)}, u32[]{:S(2)}) collective-permute-start(bf16[32,512]{1,0:T(8,128)(2,1)S(1)} %fusion.20), channel_id=1, source_target_pairs={{64,96},{65,97},{66,98},{67,99},{68,100},{69,101},{70,102},{71,103... | collective-permute-start | bytes 98312 | tf_op jit(solution)/shard_map/ppermute | solution.py:51

commit v2 on v1

--- a/solution.py
+++ b/solution.py
@@ -95,7 +95,10 @@
     step_second = jnp.where(early_core, step_other, step)
     pair = exact(step_first, step_second)
     own_map = jnp.where(early_core, step_first, pair)
-    pair_other = moved(pair.astype(jnp.bfloat16), CHIP_SWAP)
+    half_size = pair.shape[0] // 2
+    first_row = lax.axis_index("chain_2") * half_size
+    sent = lax.dynamic_slice_in_dim(pair, first_row, half_size, 0)
+    pair_got = moved(sent.astype(jnp.bfloat16), CHIP_SWAP)
 
     def added(columns, rows):
         product = jnp.dot(columns, rows, preferred_element_type=jnp.float32)
@@ -123,6 +126,9 @@
         )
         return jnp.sum(pieces.astype(jnp.float32), axis=0)
 
+    early = coupling_rows.shape[0] // 3
+    coupling_early = moved(coupling_rows[:early], BLK_SWAP)
+
     def left(rhs, factor, values):
         product = lax.dot_general(
             factor, values, (((1,), (1,)), ((), ())), preferred_element_type=jnp.float32
@@ -130,10 +136,14 @@
         return (rhs.astype(jnp.float32) - product).astype(jnp.bfloat16)
 
     width = inverse_rows.shape[0]
-    columns_own = lax.dynamic_slice_in_dim(inverse_rows, half * width, width, 1)
-    columns_other = lax.dynamic_slice_in_dim(inverse_rows, (1 - half) * width, width, 1)
-    columns_own, columns_other = lax.optimization_barrier((columns_own, columns_other))
+    columns_own = lax.optimization_barrier(
+        lax.dynamic_slice_in_dim(inverse_rows, half * width, width, 1)
+    )
     part = added(columns_own, rhs_rows)
+    inverse_rows, part = lax.optimization_barrier((inverse_rows, part))
+    columns_other = lax.optimization_barrier(
+        lax.dynamic_slice_in_dim(inverse_rows, (1 - half) * width, width, 1)
+    )
     coords = solved(part, columns_other, rhs_other)
     terms = terms_of(lax.optimization_barrier(coords))
     terms, week_rhs, pair, own_map, step_first, step_second, early_core, early_chip = (
@@ -172,7 +182,14 @@
         entering = jnp.where(early_chip, carried, exact(carried, pair_first))
         return inside + exact(entering, own_map)
 
-    pair_other, station_sum = lax.optimization_barrier((pair_other, station_sum))
+    pair_got, station_sum = lax.optimization_barrier((pair_got, station_sum))
+    pair_rest = moved(pair_got, CORE_SWAP)
+    pair_other = jnp.concatenate(
+        [
+            jnp.where(early_core, pair_got, pair_rest),
+            jnp.where(early_core, pair_rest, pair_got),
+        ]
+    )
     maps = late_maps(pair_other)
     shared = chain(exact(week_rhs - station_sum, inverse), maps)
 
@@ -180,8 +197,10 @@
     shared_all = collected(shared_low)
     later = moved(shared_low, LATER).astype(jnp.float32)
     residual_own = row_major(left(rhs_rows, coupling_rows, shared_all))
-    residual_other = moved(residual_own, BLK_SWAP)
+    residual_late = moved(row_major(residual_own[early:]), BLK_SWAP)
+    residual_early = left(rhs_other[:early], coupling_early, shared_all)
     part = added(columns_own, residual_own)
+    residual_other = jnp.concatenate([residual_early, residual_late])
     coords = solved(part, columns_other, residual_other)
     station_sum = summed(terms_of(coords))
     shared = chain(exact(week_rhs + weight * later - station_sum, inverse), maps)

time: 147 us -> 157 us (1.068)
  blocking collectives: 42 us -> 14.3 us
  starting transfers between devices: 18.4 us -> 38.9 us
  matrix products: 22.4 us -> 29.6 us
  waiting for transfers between devices: 48.4 us -> 54.4 us
  local copies, waits for them, and re-layouts: 10.7 us -> 14 us
    all_to_all x1 -> x0, blocking collectives: 15.9 us -> none  [summed(): lax.all_to_all(terms.reshape(8, samples, terms.shape[1]), REPLICAS, split...]
    all_to_all x2 -> x1, blocking collectives: 26.1 us -> 14.3 us  [collected(): lax.all_to_all(copies, REPLICAS, split_axis=0, concat_axis=0, tiled=True)]
    all_to_all x1 -> x2, starting transfers between devices: 3.41 us -> 13.1 us  [summed(): lax.all_to_all(terms.reshape(8, samples, terms.shape[1]), REPLICAS, split...]
    all_to_all x1 -> x2, waiting for transfers between devices: 6.44 us -> 14.2 us  [summed(): lax.all_to_all(terms.reshape(8, samples, terms.shape[1]), REPLICAS, split...]
    all_to_all x0 -> x1, starting transfers between devices: none -> 6.91 us  [collected(): lax.all_to_all(copies, REPLICAS, split_axis=0, concat_axis=0, tiled=True)]
    ppermute x15 -> x17, waiting for transfers between devices: 42 us -> 37.2 us  [moved(): return lax.ppermute(value, AXES, pairs)]
    ppermute x15 -> x17, starting transfers between devices: 14.9 us -> 18.9 us  [moved(): return lax.ppermute(value, AXES, pairs)]
    dynamic_slice x1, local copies, waits for them, and re-layouts: 8.03 us -> 4.8 us  [layer(): lax.dynamic_slice_in_dim(inverse_rows, (1 - half) * width, width, 1)]
  transfers between devices with their start and end apart: 16 -> 20, of which waited for: 9 -> 13; matrix products, arithmetic and copies ran while one was open for 14% -> 19% of each run, Pallas kernels for 0% -> 0%
where the time goes in v2:
time: 157 us; the launch traced here: 156 us
  waiting for transfers between devices  54.4 us (35%)
  starting transfers between devices  38.9 us (25%)
  matrix products  29.6 us (19%)
  blocking collectives  14.3 us (9%)
  local copies, waits for them, and re-layouts  14 us (9%)
  other arithmetic  3.92 us (2%)
    ppermute x17, waiting for transfers between devices, moved(): return lax.ppermute(value, AXES, pairs)  37.2 us
    ppermute x17, starting transfers between devices, moved(): return lax.ppermute(value, AXES, pairs)  18.9 us
    all_to_all x1, blocking collectives, collected(): lax.all_to_all(copies, REPLICAS, split_axis=0, concat_axis=0, tiled=True)  14.3 us
    all_to_all x2, waiting for transfers between devices, summed(): lax.all_to_all(terms.reshape(8, samples, terms.shape[1]), REPLICAS, split...  14.2 us
    all_to_all x2, starting transfers between devices, summed(): lax.all_to_all(terms.reshape(8, samples, terms.shape[1]), REPLICAS, split...  13.1 us
    dot_general x19, matrix products, exact(): return jnp.dot(left, right, precision=lax.Precision.HIGH)  11.1 us
    all_to_all x1, starting transfers between devices, collected(): lax.all_to_all(copies, REPLICAS, split_axis=0, concat_axis=0, tiled=True)  6.91 us
    dot_general x2, matrix products, added(): product = jnp.dot(columns, rows, preferred_element_type=jnp.float32)  6.33 us
  transfers between devices with their start and end apart: 20, of which 13 were waited for; matrix products, arithmetic and copies ran while one was open for 19% of the time, Pallas kernels for 0%

profile of v2, /device:TPU:96, one launch (start us, length us, event | category | flops | bytes accessed | tf_op | source)
XLA Modules:
  0.0 156.3 jit_solution(8200027745993821373)
XLA Ops:
  0.6 3.3 %collective-permute-start = (bf16[1536,256]{1,0:T(8,128)(2,1)}, bf16[1536,256]{1,0:T(8,128)(2,1)S(1)}, u32[]{:S(2)}, u32[]{:S(2)}) collective-permute-start(bf16[1536,256]{1,0:T(8,128)(2,1)} %bitcast.85), channel_id=1, source_target_pairs={{0,1},{1,0},{2,3},{3,2},{4,5},{5,4},{6,7},{7,6},{8,9},{9,8},{10,11... | collective-permute-start | bytes 2359304 | tf_op jit(solution)/shard_map/ppermute | solution.py:51
  3.9 1.4 bitcast_multiply_fusion
  5.4 2.7 %dynamic-slice_bitcast_fusion = bf16[1536,1536]{1,0:T(8,128)(2,1)S(1)} fusion(bf16[1,1,1536,3072]{3,2,1,0:T(8,128)(2,1)} %param.7, s32[]{:T(128)S(6)} %select_n.120), kind=kLoop, calls=%fused_computation | loop fusion | bytes 9437188 | tf_op jit(solution)/shard_map/dynamic_slice | solution.py:140
  8.1 2.2 %copy-done.12 = bf16[1536,1536]{1,0:T(8,128)(2,1)} copy-done((bf16[1536,1536]{1,0:T(8,128)(2,1)}, bf16[1536,1536]{1,0:T(8,128)(2,1)S(1)}, u32[]{:S(2)}) %copy-start.12) | copy-done | bytes 4718616
  10.3 2.6 %fusion.48 = f32[1536,256]{1,0:T(8,128)} fusion(bf16[1536,1536]{1,0:T(8,128)(2,1)S(1)} %dynamic-slice_bitcast_fusion, bf16[1,1,1536,256]{3,2,1,0:T(8,128)(2,1)S(1)} %copy-done.14), kind=kOutput, calls=%fused_computation.88 | convolution fusion | flops 1207959552 | bytes 7077888 | tf_op jit(solution)/shard_map/dot_general | solution.py:104
  12.9 4.8 %constant_dynamic-slice_fusion.1 = bf16[1536,1536]{1,0:T(8,128)(2,1)} fusion(bf16[1536,3072]{1,0:T(8,128)(2,1)} %bitcast.78, s32[]{:T(128)S(6)} %select_n.121), kind=kLoop, calls=%fused_computation.86 | loop fusion | bytes 9437188 | tf_op jit(solution)/shard_map/dynamic_slice | solution.py:145
  18.3 3.4 %collective-permute-done = bf16[1536,256]{1,0:T(8,128)(2,1)S(1)} collective-permute-done((bf16[1536,256]{1,0:T(8,128)(2,1)}, bf16[1536,256]{1,0:T(8,128)(2,1)S(1)}, u32[]{:S(2)}, u32[]{:S(2)}) %collective-permute-start) | collective-permute-done | bytes 786464 | tf_op jit(solution)/shard_map/ppermute | solution.py:51
  21.7 4.5 %fusion.2 = bf16[1536,256]{1,0:T(8,128)(2,1)S(1)} fusion(f32[1536,256]{1,0:T(8,128)} %fusion.48, bf16[1536,1536]{1,0:T(8,128)(2,1)} %constant_dynamic-slice_fusion.1, bf16[1536,256]{1,0:T(8,128)(2,1)S(1)} %collective-permute-done, f32[1536]{0:T(1024)S(1)} %convert_element_type.117), kind=kOutput, calls=%fused_computation.6 | convolution fusion | flops 1209139200 | bytes 7870464 | tf_op jit(solution)/shard_map/dot_general | solution.py:108
  26.3 1.3 fusion.9
  27.6 1.4 broadcast_select_fusion.1
  29.0 2.0 %broadcast_select_fusion = (f32[512,512]{1,0:T(8,128)}, f32[512,512]{1,0:T(8,128)S(1)}) fusion(f32[512,512]{1,0:T(8,128)S(1)} %get-tuple-element.22, pred[]{:T(512)S(6)} %eq.6, f32[512,512]{1,0:T(8,128)S(1)} %get-tuple-element.21), kind=kOutput, calls=%fused_computation.49 | convolution fusion | flops 805568512 | bytes 4194305 | tf_op jit(solution)/shard_map/dot_general | solution.py:55
  31.1 6.9 %all-to-all-start = ((bf16[8,32,512]{2,1,0:T(8,128)(2,1)}), bf16[8,32,512]{2,1,0:T(8,128)(2,1)S(1)}, u32[]{:S(2)}, u32[]{:S(2)}) async-start(bf16[8,32,512]{2,1,0:T(8,128)(2,1)} %bitcast.8), calls=%async_computation | async-start | bytes 524288 | tf_op jit(solution)/shard_map/all_to_all | solution.py:120
  38.0 0.8 collective-permute-start.2
  38.8 7.6 %all-to-all-done = bf16[8,32,512]{2,1,0:T(8,128)(2,1)S(1)} async-done(((bf16[8,32,512]{2,1,0:T(8,128)(2,1)}), bf16[8,32,512]{2,1,0:T(8,128)(2,1)S(1)}, u32[]{:S(2)}, u32[]{:S(2)}) %all-to-all-start) | async-done | bytes 262176 | tf_op jit(solution)/shard_map/all_to_all | solution.py:120
  46.5 1.1 collective-permute-done.2
  48.6 0.7 collective-permute-done.3
  49.7 0.8 collective-permute-start.4
  50.6 1.0 broadcast_select_fusion.4
  51.5 1.0 fusion.31
  53.0 0.7 collective-permute-done.4
  54.2 0.7 collective-permute-start.6
  55.2 0.8 collective-permute-start.7
  56.4 1.4 collective-permute-start.8
  57.8 10.0 %collective-permute-done.8 = bf16[32,512]{1,0:T(8,128)(2,1)S(1)} collective-permute-done((bf16[32,512]{1,0:T(8,128)(2,1)S(1)}, bf16[32,512]{1,0:T(8,128)(2,1)S(1)}, u32[]{:S(2)}, u32[]{:S(2)}) %collective-permute-start.8) | collective-permute-done | bytes 32800 | tf_op jit(solution)/shard_map/ppermute | solution.py:51
  69.1 0.7 broadcast_in_dim.23
  69.8 6.9 %all-to-all-start.1 = ((bf16[8,32,512]{2,1,0:T(8,128)(2,1)}), bf16[8,32,512]{2,1,0:T(8,128)(2,1)S(1)}, u32[]{:S(2)}, u32[]{:S(2)}) async-start(bf16[8,32,512]{2,1,0:T(8,128)(2,1)} %broadcast_in_dim.23), calls=%async_computation.1 | async-start | bytes 524288 | tf_op jit(solution)/shard_map/all_to_all | solution.py:60
  76.7 1.9 %slice_bitcast_fusion = bf16[512,512]{1,0:T(8,128)(2,1)} fusion(bf16[1,1,1536,512]{3,2,1,0:T(8,128)(2,1)} %param.8), kind=kLoop, calls=%fused_computation.46 | loop fusion | bytes 1048576 | tf_op jit(solution)/shard_map/slice | solution.py:130
  78.6 3.5 %collective-permute-start.9 = (bf16[512,512]{1,0:T(8,128)(2,1)}, bf16[512,512]{1,0:T(8,128)(2,1)}, u32[]{:S(2)}, u32[]{:S(2)}) collective-permute-start(bf16[512,512]{1,0:T(8,128)(2,1)} %slice_bitcast_fusion), channel_id=1, source_target_pairs={{0,1},{1,0},{2,3},{3,2},{4,5},{5,4},{6,7},{7,6},{8,9},{9,8},{10,11... | collective-permute-start | bytes 1572872 | tf_op jit(solution)/shard_map/ppermute | solution.py:51
  82.1 3.0 %all-to-all-done.1 = bf16[8,32,512]{2,1,0:T(8,128)(2,1)S(1)} async-done(((bf16[8,32,512]{2,1,0:T(8,128)(2,1)}), bf16[8,32,512]{2,1,0:T(8,128)(2,1)S(1)}, u32[]{:S(2)}, u32[]{:S(2)}) %all-to-all-start.1) | async-done | bytes 262176 | tf_op jit(solution)/shard_map/all_to_all | solution.py:60
  85.2 2.2 %fusion.3 = bf16[1536,256]{1,0:T(8,128)(2,1)S(1)} fusion(bf16[256,512]{1,0:T(8,128)(2,1)S(1)} %bitcast.81, bf16[1,1,1536,512]{3,2,1,0:T(8,128)(2,1)} %param.8, bf16[1,1,1536,256]{3,2,1,0:T(8,128)(2,1)} %param.9), kind=kOutput, calls=%fused_computation.7 | convolution fusion | flops 403832832 | bytes 3407872 | tf_op jit(solution)/shard_map/dot_general | solution.py:133
  87.4 1.5 collective-permute-start.10
  88.9 3.7 %fusion.56 = f32[1536,256]{1,0:T(8,128)S(1)} fusion(bf16[1536,1536]{1,0:T(8,128)(2,1)} %copy-done.12, bf16[1536,256]{1,0:T(8,128)(2,1)S(1)} %fusion.3), kind=kOutput, calls=%fused_computation.96 | convolution fusion | flops 1207959552 | bytes 7077888 | tf_op jit(solution)/shard_map/dot_general | solution.py:104
  92.7 3.4 %collective-permute-done.9 = bf16[512,512]{1,0:T(8,128)(2,1)} collective-permute-done((bf16[512,512]{1,0:T(8,128)(2,1)}, bf16[512,512]{1,0:T(8,128)(2,1)}, u32[]{:S(2)}, u32[]{:S(2)}) %collective-permute-start.9) | collective-permute-done | bytes 524320 | tf_op jit(solution)/shard_map/ppermute | solution.py:51
  96.1 1.4 subtract_convert_fusion
  97.5 6.0 %collective-permute-done.10 = bf16[1024,256]{1,0:T(8,128)(2,1)S(1)} collective-permute-done((bf16[1024,256]{1,0:T(8,128)(2,1)S(1)}, bf16[1024,256]{1,0:T(8,128)(2,1)S(1)}, u32[]{:S(2)}, u32[]{:S(2)}) %collective-permute-start.10) | collective-permute-done | bytes 524320 | tf_op jit(solution)/shard_map/ppermute | solution.py:51
  103.6 1.4 fusion.1
  105.0 1.3 fusion.12
  106.4 6.1 %all-to-all-start.2 = ((bf16[8,32,512]{2,1,0:T(8,128)(2,1)}), bf16[8,32,512]{2,1,0:T(8,128)(2,1)S(1)}, u32[]{:S(2)}, u32[]{:S(2)}) async-start(bf16[8,32,512]{2,1,0:T(8,128)(2,1)} %bitcast.84), calls=%async_computation.2 | async-start | bytes 524288 | tf_op jit(solution)/shard_map/all_to_all | solution.py:120
  112.5 1.9 %collective-permute-start.11 = (bf16[32,512]{1,0:T(8,128)(2,1)}, bf16[32,512]{1,0:T(8,128)(2,1)}, u32[]{:S(2)}, u32[]{:S(2)}) collective-permute-start(bf16[32,512]{1,0:T(8,128)(2,1)} %copy-done.15), channel_id=1, source_target_pairs={{8,0},{9,1},{10,2},{11,3},{12,4},{13,5},{14,6},{15,7},{16,8},{17,9... | collective-permute-start | bytes 98312 | tf_op jit(solution)/shard_map/ppermute | solution.py:51
  114.4 6.5 %all-to-all-done.2 = bf16[8,32,512]{2,1,0:T(8,128)(2,1)S(1)} async-done(((bf16[8,32,512]{2,1,0:T(8,128)(2,1)}), bf16[8,32,512]{2,1,0:T(8,128)(2,1)S(1)}, u32[]{:S(2)}, u32[]{:S(2)}) %all-to-all-start.2) | async-done | bytes 262176 | tf_op jit(solution)/shard_map/all_to_all | solution.py:120
  121.0 1.7 %fusion.21 = f32[32,512]{1,0:T(8,128)S(1)} fusion(f32[1,512,512]{2,1,0:T(8,128)} %param.11, f32[32,512]{1,0:T(8,128)S(1)} %convert_reduce_fusion, f32[32,512]{1,0:T(8,128)S(1)} %bitcast.87, bf16[32,512]{1,0:T(8,128)(2,1)} %collective-permute-done.11, f32[512]{0:T(512)S(1)} %copy-done.17), kind=kOutput, calls=%fused_computation.32 | convolution fusion | flops 50397184 | bytes 1280000 | tf_op jit(solution)/shard_map/dot_general | solution.py:55
  122.8 1.2 collective-permute-done.12
  125.1 3.4 %collective-permute-done.13 = bf16[32,512]{1,0:T(8,128)(2,1)S(1)} collective-permute-done((bf16[32,512]{1,0:T(8,128)(2,1)S(1)}, bf16[32,512]{1,0:T(8,128)(2,1)S(1)}, u32[]{:S(2)}, u32[]{:S(2)}) %collective-permute-start.13) | collective-permute-done | bytes 32800 | tf_op jit(solution)/shard_map/ppermute | solution.py:51
  129.9 0.8 collective-permute-start.15
  131.2 1.4 collective-permute-start.16
  132.6 7.1 %collective-permute-done.16 = bf16[32,512]{1,0:T(8,128)(2,1)S(1)} collective-permute-done((bf16[32,512]{1,0:T(8,128)(2,1)S(1)}, bf16[32,512]{1,0:T(8,128)(2,1)S(1)}, u32[]{:S(2)}, u32[]{:S(2)}) %collective-permute-start.16) | collective-permute-done | bytes 32800 | tf_op jit(solution)/shard_map/ppermute | solution.py:51
  141.0 14.3 %all_to_all.20 = bf16[8,32,512]{2,1,0:T(8,128)(2,1)S(1)} all-to-all(bf16[8,32,512]{2,1,0:T(8,128)(2,1)S(1)} %broadcast_in_dim.25), channel_id=1, replica_groups=mesh['chain_0'=4,'chain_1'=2,'chain_2'=2,'tech'=4,'blk'=2] {'tech','blk'}, dimensions={0} | all-to-all | bytes 524288 | tf_op jit(solution)/shard_map/all_to_all | solution.py:60
  155.3 1.0 copy.12
  (82 shorter events, 9.3 us)
Async XLA Ops:
  0.6 17.4 %copy-start = (f32[1,512,256]{2,1,0:T(8,128)S(1)}, f32[1,512,256]{2,1,0:T(8,128)}, u32[]{:S(2)}) copy-start(f32[1,512,256]{2,1,0:T(8,128)} %param.13) | copy-start | bytes 1572868
  0.6 21.1 %collective-permute-start = (bf16[1536,256]{1,0:T(8,128)(2,1)}, bf16[1536,256]{1,0:T(8,128)(2,1)S(1)}, u32[]{:S(2)}, u32[]{:S(2)}) collective-permute-start(bf16[1536,256]{1,0:T(8,128)(2,1)} %bitcast.85), channel_id=1, source_target_pairs={{0,1},{1,0},{2,3},{3,2},{4,5},{5,4},{6,7},{7,6},{8,9},{9,8},{10,11... | collective-permute-start | bytes 2359304 | tf_op jit(solution)/shard_map/ppermute | solution.py:51
  5.3 22.3 %collective-permute-start.1 = (f32[512,512]{1,0:T(8,128)S(1)}, f32[512,512]{1,0:T(8,128)}, u32[]{:S(2)}, u32[]{:S(2)}) collective-permute-start(f32[512,512]{1,0:T(8,128)S(1)} %bitcast_multiply_fusion), channel_id=1, source_target_pairs={{0,8},{1,9},{2,10},{3,11},{4,12},{5,13},{6,14},{7,15},{8,0},{9,1},... | collective-permute-start | bytes 3145736 | tf_op jit(solution)/shard_map/ppermute | solution.py:51
  5.4 4.9 %copy-start.14 = (bf16[1,1,1536,256]{3,2,1,0:T(8,128)(2,1)S(1)}, bf16[1,1,1536,256]{3,2,1,0:T(8,128)(2,1)}, u32[]{:S(2)}) copy-start(bf16[1,1,1536,256]{3,2,1,0:T(8,128)(2,1)} %param.9) | copy-start | bytes 2359300
  8.1 2.2 %copy-start.12 = (bf16[1536,1536]{1,0:T(8,128)(2,1)}, bf16[1536,1536]{1,0:T(8,128)(2,1)S(1)}, u32[]{:S(2)}) copy-start(bf16[1536,1536]{1,0:T(8,128)(2,1)S(1)} %dynamic-slice_bitcast_fusion) | copy-start | bytes 14155780
  12.9 4.8 %copy-start.18 = (s32[1,1,512]{2,1,0:T(1,128)S(1)}, s32[1,1,512]{2,1,0:T(1,128)}, u32[]{:S(2)}) copy-start(s32[1,1,512]{2,1,0:T(1,128)} %param.10) | copy-start | bytes 6148
  18.3 7.9 %copy-start.1 = (bf16[1,1,1536,512]{3,2,1,0:T(8,128)(2,1)S(1)}, bf16[1,1,1536,512]{3,2,1,0:T(8,128)(2,1)}, u32[]{:S(2)}) copy-start(bf16[1,1,1536,512]{3,2,1,0:T(8,128)(2,1)} %param.8) | copy-start | bytes 4718596
  21.7 4.5 %copy-start.16 = (bf16[1536,256]{1,0:T(8,128)(2,1)}, bf16[1536,256]{1,0:T(8,128)(2,1)S(1)}, u32[]{:S(2)}) copy-start(bf16[1536,256]{1,0:T(8,128)(2,1)S(1)} %collective-permute-done) | copy-start | bytes 2359300
  26.2 1.3 copy-start.3
  26.3 1.3 copy-start.17
  29.0 2.0 %copy-start.4 = (f32[512,512]{1,0:T(8,128)}, f32[512,512]{1,0:T(8,128)S(1)}, u32[]{:S(2)}) copy-start(f32[512,512]{1,0:T(8,128)S(1)} %get-tuple-element.22) | copy-start | bytes 3145732
  29.0 2.0 %copy-start.7 = (f32[512,512]{1,0:T(8,128)}, f32[512,512]{1,0:T(8,128)S(1)}, u32[]{:S(2)}) copy-start(f32[512,512]{1,0:T(8,128)S(1)} %get-tuple-element.21) | copy-start | bytes 3145732
  31.1 15.4 %all-to-all-start = ((bf16[8,32,512]{2,1,0:T(8,128)(2,1)}), bf16[8,32,512]{2,1,0:T(8,128)(2,1)S(1)}, u32[]{:S(2)}, u32[]{:S(2)}) async-start(bf16[8,32,512]{2,1,0:T(8,128)(2,1)} %bitcast.8), calls=%async_computation | async-start | bytes 524288 | tf_op jit(solution)/shard_map/all_to_all | solution.py:120
  38.0 9.5 %collective-permute-start.2 = (bf16[256,512]{1,0:T(8,128)(2,1)S(1)}, bf16[256,512]{1,0:T(8,128)(2,1)}, u32[]{:S(2)}, u32[]{:S(2)}) collective-permute-start(bf16[256,512]{1,0:T(8,128)(2,1)S(1)} %dynamic-slice_convert_fusion), channel_id=1, source_target_pairs={{0,16},{1,17},{2,18},{3,19},{4,20},{5,21},{6,22},{7,23},{8,24},{9,... | collective-permute-start | bytes 786440 | tf_op jit(solution)/shard_map/ppermute | solution.py:51
  46.4 2.9 %copy-start.8 = (f32[512,512]{1,0:T(8,128)S(1)}, f32[512,512]{1,0:T(8,128)}, u32[]{:S(2)}) copy-start(f32[512,512]{1,0:T(8,128)} %copy-done.7) | copy-start | bytes 3145732
  48.0 1.3 collective-permute-start.3
  48.1 2.5 %collective-permute-start.5 = (bf16[256,512]{1,0:T(8,128)(2,1)}, bf16[256,512]{1,0:T(8,128)(2,1)S(1)}, u32[]{:S(2)}, u32[]{:S(2)}) collective-permute-start(bf16[256,512]{1,0:T(8,128)(2,1)} %collective-permute-done.2), channel_id=1, source_target_pairs={{0,8},{1,9},{2,10},{3,11},{4,12},{5,13},{6,14},{7,15},{8,0},{9,1},... | collective-permute-start | bytes 786440 | tf_op jit(solution)/shard_map/ppermute | solution.py:51
  49.7 4.0 %collective-permute-start.4 = (bf16[32,512]{1,0:T(8,128)(2,1)S(1)}, bf16[32,512]{1,0:T(8,128)(2,1)S(1)}, u32[]{:S(2)}, u32[]{:S(2)}) collective-permute-start(bf16[32,512]{1,0:T(8,128)(2,1)S(1)} %get-tuple-element.34), channel_id=1, source_target_pairs={{0,16},{1,17},{2,18},{3,19},{4,20},{5,21},{6,22},{7,23},{8,24},{9,... | collective-permute-start | bytes 98312 | tf_op jit(solution)/shard_map/ppermute | solution.py:51
  54.2 0.7 collective-permute-start.6
  55.2 13.1 %copy-start.10 = (f32[512,512]{1,0:T(8,128)S(1)}, f32[512,512]{1,0:T(8,128)}, u32[]{:S(2)}) copy-start(f32[512,512]{1,0:T(8,128)} %get-tuple-element.25) | copy-start | bytes 3145732
  55.2 0.8 collective-permute-start.7
  56.4 12.3 %copy-start.5 = (f32[512,512]{1,0:T(8,128)S(1)}, f32[512,512]{1,0:T(8,128)}, u32[]{:S(2)}) copy-start(f32[512,512]{1,0:T(8,128)} %copy-done.4) | copy-start | bytes 3145732
  56.4 11.4 %collective-permute-start.8 = (bf16[32,512]{1,0:T(8,128)(2,1)S(1)}, bf16[32,512]{1,0:T(8,128)(2,1)S(1)}, u32[]{:S(2)}, u32[]{:S(2)}) collective-permute-start(bf16[32,512]{1,0:T(8,128)(2,1)S(1)} %fusion.18), channel_id=1, source_target_pairs={{64,96},{65,97},{66,98},{67,99},{68,100},{69,101},{70,102},{71,103... | collective-permute-start | bytes 98312 | tf_op jit(solution)/shard_map/ppermute | solution.py:51
  69.1 0.7 copy-start.15
  69.8 15.3 %all-to-all-start.1 = ((bf16[8,32,512]{2,1,0:T(8,128)(2,1)}), bf16[8,32,512]{2,1,0:T(8,128)(2,1)S(1)}, u32[]{:S(2)}, u32[]{:S(2)}) async-start(bf16[8,32,512]{2,1,0:T(8,128)(2,1)} %broadcast_in_dim.23), calls=%async_computation.1 | async-start | bytes 524288 | tf_op jit(solution)/shard_map/all_to_all | solution.py:60
  78.6 17.5 %collective-permute-start.9 = (bf16[512,512]{1,0:T(8,128)(2,1)}, bf16[512,512]{1,0:T(8,128)(2,1)}, u32[]{:S(2)}, u32[]{:S(2)}) collective-permute-start(bf16[512,512]{1,0:T(8,128)(2,1)} %slice_bitcast_fusion), channel_id=1, source_target_pairs={{0,1},{1,0},{2,3},{3,2},{4,5},{5,4},{6,7},{7,6},{8,9},{9,8},{10,11... | collective-permute-start | bytes 1572872 | tf_op jit(solution)/shard_map/ppermute | solution.py:51
  87.4 16.2 %slice-start = ((s8[4718592]{0:T(1024)(128)(4,1)}), s8[4194304]{0:T(1024)(128)(4,1)S(1)}, s32[]{:S(2)}) async-start(s8[4718592]{0:T(1024)(128)(4,1)} %bitcast.79), calls=%async_computation.4 | async-start | bytes 8388608
  87.4 16.1 %slice-start.1 = ((s8[4718592]{0:T(1024)(128)(4,1)}), s8[524288]{0:T(1024)(128)(4,1)S(1)}, s32[]{:S(2)}) async-start(s8[4718592]{0:T(1024)(128)(4,1)} %bitcast.79), calls=%async_computation.5 | async-start | bytes 1048576
  87.4 16.1 %collective-permute-start.10 = (bf16[1024,256]{1,0:T(8,128)(2,1)S(1)}, bf16[1024,256]{1,0:T(8,128)(2,1)S(1)}, u32[]{:S(2)}, u32[]{:S(2)}) collective-permute-start(bf16[1024,256]{1,0:T(8,128)(2,1)S(1)} %slice.17), channel_id=1, source_target_pairs={{0,1},{1,0},{2,3},{3,2},{4,5},{5,4},{6,7},{7,6},{8,9},{9,8},{10,11... | collective-permute-start | bytes 1572872 | tf_op jit(solution)/shard_map/ppermute | solution.py:51
  97.5 7.5 %copy-start.2 = (bf16[1,1,1536,512]{3,2,1,0:T(8,128)(2,1)S(1)}, bf16[1,1,1536,512]{3,2,1,0:T(8,128)(2,1)}, u32[]{:S(2)}) copy-start(bf16[1,1,1536,512]{3,2,1,0:T(8,128)(2,1)} %param.8) | copy-start | bytes 4718596
  105.0 1.3 copy-start.13
  106.4 14.6 %all-to-all-start.2 = ((bf16[8,32,512]{2,1,0:T(8,128)(2,1)}), bf16[8,32,512]{2,1,0:T(8,128)(2,1)S(1)}, u32[]{:S(2)}, u32[]{:S(2)}) async-start(bf16[8,32,512]{2,1,0:T(8,128)(2,1)} %bitcast.84), calls=%async_computation.2 | async-start | bytes 524288 | tf_op jit(solution)/shard_map/all_to_all | solution.py:120
  112.5 8.5 %collective-permute-start.11 = (bf16[32,512]{1,0:T(8,128)(2,1)}, bf16[32,512]{1,0:T(8,128)(2,1)}, u32[]{:S(2)}, u32[]{:S(2)}) collective-permute-start(bf16[32,512]{1,0:T(8,128)(2,1)} %copy-done.15), channel_id=1, source_target_pairs={{8,0},{9,1},{10,2},{11,3},{12,4},{13,5},{14,6},{15,7},{16,8},{17,9... | collective-permute-start | bytes 98312 | tf_op jit(solution)/shard_map/ppermute | solution.py:51
  120.9 3.1 %copy-start.9 = (f32[512,512]{1,0:T(8,128)S(1)}, f32[512,512]{1,0:T(8,128)}, u32[]{:S(2)}) copy-start(f32[512,512]{1,0:T(8,128)} %copy-done.7) | copy-start | bytes 3145732
  122.7 1.3 collective-permute-start.12
  124.5 4.0 %collective-permute-start.13 = (bf16[32,512]{1,0:T(8,128)(2,1)S(1)}, bf16[32,512]{1,0:T(8,128)(2,1)S(1)}, u32[]{:S(2)}, u32[]{:S(2)}) collective-permute-start(bf16[32,512]{1,0:T(8,128)(2,1)S(1)} %get-tuple-element.38), channel_id=1, source_target_pairs={{0,16},{1,17},{2,18},{3,19},{4,20},{5,21},{6,22},{7,23},{8,24},{9,... | collective-permute-start | bytes 98312 | tf_op jit(solution)/shard_map/ppermute | solution.py:51
  128.9 0.7 collective-permute-start.14
  129.9 10.2 %copy-start.11 = (f32[512,512]{1,0:T(8,128)S(1)}, f32[512,512]{1,0:T(8,128)}, u32[]{:S(2)}) copy-start(f32[512,512]{1,0:T(8,128)} %get-tuple-element.25) | copy-start | bytes 3145732
  129.9 0.8 collective-permute-start.15
  131.2 9.4 %copy-start.6 = (f32[512,512]{1,0:T(8,128)S(1)}, f32[512,512]{1,0:T(8,128)}, u32[]{:S(2)}) copy-start(f32[512,512]{1,0:T(8,128)} %copy-done.4) | copy-start | bytes 3145732
  131.2 8.5 %collective-permute-start.16 = (bf16[32,512]{1,0:T(8,128)(2,1)S(1)}, bf16[32,512]{1,0:T(8,128)(2,1)S(1)}, u32[]{:S(2)}, u32[]{:S(2)}) collective-permute-start(bf16[32,512]{1,0:T(8,128)(2,1)S(1)} %fusion.20), channel_id=1, source_target_pairs={{64,96},{65,97},{66,98},{67,99},{68,100},{69,101},{70,102},{71,103... | collective-permute-start | bytes 98312 | tf_op jit(solution)/shard_map/ppermute | solution.py:51

commit v3 on v2

--- a/solution.py
+++ b/solution.py
@@ -126,8 +126,10 @@
         )
         return jnp.sum(pieces.astype(jnp.float32), axis=0)
 
-    early = coupling_rows.shape[0] // 3
-    coupling_early = moved(coupling_rows[:early], BLK_SWAP)
+    first_rows = coupling_rows.shape[0] // 8
+    early = first_rows + coupling_rows.shape[0] // 3
+    coupling_first = moved(coupling_rows[:first_rows], BLK_SWAP)
+    coupling_next = moved(coupling_rows[first_rows:early], BLK_SWAP)
 
     def left(rhs, factor, values):
         product = lax.dot_general(
@@ -136,9 +138,7 @@
         return (rhs.astype(jnp.float32) - product).astype(jnp.bfloat16)
 
     width = inverse_rows.shape[0]
-    columns_own = lax.optimization_barrier(
-        lax.dynamic_slice_in_dim(inverse_rows, half * width, width, 1)
-    )
+    columns_own = lax.dynamic_slice_in_dim(inverse_rows, half * width, width, 1)
     part = added(columns_own, rhs_rows)
     inverse_rows, part = lax.optimization_barrier((inverse_rows, part))
     columns_other = lax.optimization_barrier(
@@ -198,6 +198,7 @@
     later = moved(shared_low, LATER).astype(jnp.float32)
     residual_own = row_major(left(rhs_rows, coupling_rows, shared_all))
     residual_late = moved(row_major(residual_own[early:]), BLK_SWAP)
+    coupling_early = jnp.concatenate([coupling_first, coupling_next])
     residual_early = left(rhs_other[:early], coupling_early, shared_all)
     part = added(columns_own, residual_own)
     residual_other = jnp.concatenate([residual_early, residual_late])

time: 157 us -> 156 us (level)
  starting transfers between devices: 38.9 us -> 42.1 us
  local copies, waits for them, and re-layouts: 14 us -> 10.8 us
  matrix products: 29.6 us -> 32.1 us
  waiting for transfers between devices: 54.4 us -> 52 us
    ppermute x17 -> x18, starting transfers between devices: 18.9 us -> 22.1 us  [moved(): return lax.ppermute(value, AXES, pairs)]
    dynamic_slice x1 -> x0, local copies, waits for them, and re-layouts: 2.72 us -> none  [layer(): lax.dynamic_slice_in_dim(inverse_rows, half * width, width, 1)]
    ppermute x17 -> x18, waiting for transfers between devices: 37.2 us -> 34.8 us  [moved(): return lax.ppermute(value, AXES, pairs)]
    dot_general x2, matrix products: 6.33 us -> 8.62 us  [added(): product = jnp.dot(columns, rows, preferred_element_type=jnp.float32)]
    unnamed x43 -> x41, local copies, waits for them, and re-layouts: 3.26 us -> 1.1 us
    slice x1 -> x2, local copies, waits for them, and re-layouts: 1.87 us -> 3.48 us  [the longest x1 1.87 us: layer(): coupling_next = moved(coupling_rows[first_rows:early], BLK_SWAP)]
  transfers between devices with their start and end apart: 20 -> 21, of which waited for: 13 -> 13; matrix products, arithmetic and copies ran while one was open for 19% -> 22% of each run, Pallas kernels for 0% -> 0%
where the time goes in v3:
time: 156 us; the launch traced here: 155 us
  waiting for transfers between devices  52 us (33%)
  starting transfers between devices  42.1 us (27%)
  matrix products  32.1 us (21%)
  blocking collectives  12.8 us (8%)
  local copies, waits for them, and re-layouts  10.8 us (7%)
  other arithmetic  3.92 us (3%)
    ppermute x18, waiting for transfers between devices, moved(): return lax.ppermute(value, AXES, pairs)  34.8 us
    ppermute x18, starting transfers between devices, moved(): return lax.ppermute(value, AXES, pairs)  22.1 us
    all_to_all x2, waiting for transfers between devices, summed(): lax.all_to_all(terms.reshape(8, samples, terms.shape[1]), REPLICAS, split...  14.2 us
    all_to_all x2, starting transfers between devices, summed(): lax.all_to_all(terms.reshape(8, samples, terms.shape[1]), REPLICAS, split...  13.1 us
    all_to_all x1, blocking collectives, collected(): lax.all_to_all(copies, REPLICAS, split_axis=0, concat_axis=0, tiled=True)  12.8 us
    dot_general x19, matrix products, exact(): return jnp.dot(left, right, precision=lax.Precision.HIGH)  11.1 us
    dot_general x2, matrix products, added(): product = jnp.dot(columns, rows, preferred_element_type=jnp.float32)  8.62 us
    all_to_all x1, starting transfers between devices, collected(): lax.all_to_all(copies, REPLICAS, split_axis=0, concat_axis=0, tiled=True)  6.9 us
  transfers between devices with their start and end apart: 21, of which 13 were waited for; matrix products, arithmetic and copies ran while one was open for 22% of the time, Pallas kernels for 0%

profile of v3, /device:TPU:96, one launch (start us, length us, event | category | flops | bytes accessed | tf_op | source)
XLA Modules:
  0.0 155.0 jit_solution(3191294367753024911)
XLA Ops:
  0.7 3.3 %collective-permute-start = (bf16[1536,256]{1,0:T(8,128)(2,1)}, bf16[1536,256]{1,0:T(8,128)(2,1)S(1)}, u32[]{:S(2)}, u32[]{:S(2)}) collective-permute-start(bf16[1536,256]{1,0:T(8,128)(2,1)} %bitcast.85), channel_id=1, source_target_pairs={{0,1},{1,0},{2,3},{3,2},{4,5},{5,4},{6,7},{7,6},{8,9},{9,8},{10,11... | collective-permute-start | bytes 2359304 | tf_op jit(solution)/shard_map/ppermute | solution.py:51
  3.9 1.4 bitcast_multiply_fusion
  5.4 4.9 %fusion.2 = f32[1536,256]{1,0:T(8,128)} fusion(bf16[1,1,1536,3072]{3,2,1,0:T(8,128)(2,1)} %param.7, s32[]{:T(128)S(6)} %select_n.120, bf16[1,1,1536,256]{3,2,1,0:T(8,128)(2,1)S(1)} %copy-done.13), kind=kOutput, calls=%fused_computation.2 | convolution fusion | flops 1207959552 | bytes 7077892 | tf_op jit(solution)/shard_map/dot_general | solution.py:104
  10.3 4.8 %constant_dynamic-slice_fusion.1 = bf16[1536,1536]{1,0:T(8,128)(2,1)} fusion(bf16[1536,3072]{1,0:T(8,128)(2,1)} %bitcast.80, s32[]{:T(128)S(6)} %select_n.121), kind=kLoop, calls=%fused_computation.96 | loop fusion | bytes 9437188 | tf_op jit(solution)/shard_map/dynamic_slice | solution.py:145
  15.7 6.0 %collective-permute-done = bf16[1536,256]{1,0:T(8,128)(2,1)S(1)} collective-permute-done((bf16[1536,256]{1,0:T(8,128)(2,1)}, bf16[1536,256]{1,0:T(8,128)(2,1)S(1)}, u32[]{:S(2)}, u32[]{:S(2)}) %collective-permute-start) | collective-permute-done | bytes 786464 | tf_op jit(solution)/shard_map/ppermute | solution.py:51
  21.7 4.5 %fusion.8 = bf16[1536,256]{1,0:T(8,128)(2,1)S(1)} fusion(f32[1536,256]{1,0:T(8,128)} %fusion.2, bf16[1536,1536]{1,0:T(8,128)(2,1)} %constant_dynamic-slice_fusion.1, bf16[1536,256]{1,0:T(8,128)(2,1)S(1)} %collective-permute-done, f32[1536]{0:T(1024)S(1)} %convert_element_type.117), kind=kOutput, calls=%fused_computation.11 | convolution fusion | flops 1209139200 | bytes 7870464 | tf_op jit(solution)/shard_map/dot_general | solution.py:108
  26.3 1.3 fusion.15
  27.6 1.4 broadcast_select_fusion.1
  29.0 2.1 %broadcast_select_fusion = (f32[512,512]{1,0:T(8,128)}, f32[512,512]{1,0:T(8,128)S(1)}) fusion(f32[512,512]{1,0:T(8,128)S(1)} %get-tuple-element.22, pred[]{:T(512)S(6)} %eq.6, f32[512,512]{1,0:T(8,128)S(1)} %get-tuple-element.21), kind=kOutput, calls=%fused_computation.57 | convolution fusion | flops 805568512 | bytes 4194305 | tf_op jit(solution)/shard_map/dot_general | solution.py:55
  31.1 6.9 %all-to-all-start = ((bf16[8,32,512]{2,1,0:T(8,128)(2,1)}), bf16[8,32,512]{2,1,0:T(8,128)(2,1)S(1)}, u32[]{:S(2)}, u32[]{:S(2)}) async-start(bf16[8,32,512]{2,1,0:T(8,128)(2,1)} %bitcast.8), calls=%async_computation | async-start | bytes 524288 | tf_op jit(solution)/shard_map/all_to_all | solution.py:120
  38.1 0.8 collective-permute-start.2
  38.8 7.6 %all-to-all-done = bf16[8,32,512]{2,1,0:T(8,128)(2,1)S(1)} async-done(((bf16[8,32,512]{2,1,0:T(8,128)(2,1)}), bf16[8,32,512]{2,1,0:T(8,128)(2,1)S(1)}, u32[]{:S(2)}, u32[]{:S(2)}) %all-to-all-start) | async-done | bytes 262176 | tf_op jit(solution)/shard_map/all_to_all | solution.py:120
  46.5 1.1 collective-permute-done.2
  48.6 0.7 collective-permute-done.3
  49.8 0.8 collective-permute-start.4
  50.6 1.0 broadcast_select_fusion.4
  51.6 1.0 fusion.41
  53.1 0.7 collective-permute-done.4
  54.2 0.7 collective-permute-start.6
  55.2 0.8 collective-permute-start.7
  56.5 1.4 collective-permute-start.8
  57.9 1.6 %slice_bitcast_fusion.1 = bf16[192,512]{1,0:T(8,128)(2,1)} fusion(bf16[1,1,1536,512]{3,2,1,0:T(8,128)(2,1)} %param.8), kind=kLoop, calls=%fused_computation.65 | loop fusion | bytes 393216 | tf_op jit(solution)/shard_map/slice | solution.py:131
  59.5 3.2 %collective-permute-start.9 = (bf16[192,512]{1,0:T(8,128)(2,1)}, bf16[192,512]{1,0:T(8,128)(2,1)}, u32[]{:S(2)}, u32[]{:S(2)}) collective-permute-start(bf16[192,512]{1,0:T(8,128)(2,1)} %slice_bitcast_fusion.1), channel_id=1, source_target_pairs={{0,1},{1,0},{2,3},{3,2},{4,5},{5,4},{6,7},{7,6},{8,9},{9,8},{10,11... | collective-permute-start | bytes 589832 | tf_op jit(solution)/shard_map/ppermute | solution.py:51
  62.8 5.1 %collective-permute-done.8 = bf16[32,512]{1,0:T(8,128)(2,1)S(1)} collective-permute-done((bf16[32,512]{1,0:T(8,128)(2,1)S(1)}, bf16[32,512]{1,0:T(8,128)(2,1)S(1)}, u32[]{:S(2)}, u32[]{:S(2)}) %collective-permute-start.8) | collective-permute-done | bytes 32800 | tf_op jit(solution)/shard_map/ppermute | solution.py:51
  69.1 0.7 broadcast_in_dim.23
  69.9 6.9 %all-to-all-start.1 = ((bf16[8,32,512]{2,1,0:T(8,128)(2,1)}), bf16[8,32,512]{2,1,0:T(8,128)(2,1)S(1)}, u32[]{:S(2)}, u32[]{:S(2)}) async-start(bf16[8,32,512]{2,1,0:T(8,128)(2,1)} %broadcast_in_dim.23), calls=%async_computation.1 | async-start | bytes 524288 | tf_op jit(solution)/shard_map/all_to_all | solution.py:60
  76.8 1.9 %slice_bitcast_fusion = bf16[512,512]{1,0:T(8,128)(2,1)} fusion(bf16[1,1,1536,512]{3,2,1,0:T(8,128)(2,1)} %param.8), kind=kLoop, calls=%fused_computation.54 | loop fusion | bytes 1048576 | tf_op jit(solution)/shard_map/slice | solution.py:132
  78.6 3.5 %collective-permute-start.10 = (bf16[512,512]{1,0:T(8,128)(2,1)}, bf16[512,512]{1,0:T(8,128)(2,1)}, u32[]{:S(2)}, u32[]{:S(2)}) collective-permute-start(bf16[512,512]{1,0:T(8,128)(2,1)} %slice_bitcast_fusion), channel_id=1, source_target_pairs={{0,1},{1,0},{2,3},{3,2},{4,5},{5,4},{6,7},{7,6},{8,9},{9,8},{10,11... | collective-permute-start | bytes 1572872 | tf_op jit(solution)/shard_map/ppermute | solution.py:51
  82.2 3.0 %all-to-all-done.1 = bf16[8,32,512]{2,1,0:T(8,128)(2,1)S(1)} async-done(((bf16[8,32,512]{2,1,0:T(8,128)(2,1)}), bf16[8,32,512]{2,1,0:T(8,128)(2,1)S(1)}, u32[]{:S(2)}, u32[]{:S(2)}) %all-to-all-start.1) | async-done | bytes 262176 | tf_op jit(solution)/shard_map/all_to_all | solution.py:60
  85.2 2.2 %fusion.9 = bf16[1536,256]{1,0:T(8,128)(2,1)S(1)} fusion(bf16[256,512]{1,0:T(8,128)(2,1)S(1)} %bitcast.82, bf16[1,1,1536,512]{3,2,1,0:T(8,128)(2,1)} %param.8, bf16[1,1,1536,256]{3,2,1,0:T(8,128)(2,1)} %param.9), kind=kOutput, calls=%fused_computation.12 | convolution fusion | flops 403832832 | bytes 3407872 | tf_op jit(solution)/shard_map/dot_general | solution.py:135
  87.5 1.5 collective-permute-start.11
  89.0 3.7 %fusion = f32[1536,256]{1,0:T(8,128)S(1)} fusion(bf16[1536,256]{1,0:T(8,128)(2,1)S(1)} %fusion.9, bf16[1,1,1536,3072]{3,2,1,0:T(8,128)(2,1)} %param.7, s32[]{:T(128)S(6)} %select_n.120), kind=kOutput, calls=%fused_computation | convolution fusion | flops 1207959552 | bytes 7077892 | tf_op jit(solution)/shard_map/dot_general | solution.py:104
  92.7 3.4 %collective-permute-done.10 = bf16[512,512]{1,0:T(8,128)(2,1)} collective-permute-done((bf16[512,512]{1,0:T(8,128)(2,1)}, bf16[512,512]{1,0:T(8,128)(2,1)}, u32[]{:S(2)}, u32[]{:S(2)}) %collective-permute-start.10) | collective-permute-done | bytes 524320 | tf_op jit(solution)/shard_map/ppermute | solution.py:51
  96.1 1.6 %subtract_convert_fusion = bf16[704,256]{1,0:T(8,128)(2,1)S(1)} fusion(bf16[1536,256]{1,0:T(8,128)(2,1)} %copy-done.17, bf16[256,512]{1,0:T(8,128)(2,1)S(1)} %bitcast.83, bf16[512,512]{1,0:T(8,128)(2,1)} %collective-permute-done.10, bf16[192,512]{1,0:T(8,128)(2,1)} %collective-permute-done.9), kind=kOutput, calls=%fused_computation.50 | convolution fusion | flops 186531840 | bytes 1703936 | tf_op jit(solution)/shard_map/dot_general | solution.py:135
  97.8 3.7 %collective-permute-done.11 = bf16[832,256]{1,0:T(8,128)(2,1)S(1)} collective-permute-done((bf16[832,256]{1,0:T(8,128)(2,1)S(1)}, bf16[832,256]{1,0:T(8,128)(2,1)S(1)}, u32[]{:S(2)}, u32[]{:S(2)}) %collective-permute-start.11) | collective-permute-done | bytes 426016 | tf_op jit(solution)/shard_map/ppermute | solution.py:51
  101.5 1.4 fusion.7
  103.0 1.3 fusion.18
  104.3 6.2 %all-to-all-start.2 = ((bf16[8,32,512]{2,1,0:T(8,128)(2,1)}), bf16[8,32,512]{2,1,0:T(8,128)(2,1)S(1)}, u32[]{:S(2)}, u32[]{:S(2)}) async-start(bf16[8,32,512]{2,1,0:T(8,128)(2,1)} %bitcast.84), calls=%async_computation.2 | async-start | bytes 524288 | tf_op jit(solution)/shard_map/all_to_all | solution.py:120
  110.5 1.9 %collective-permute-start.12 = (bf16[32,512]{1,0:T(8,128)(2,1)}, bf16[32,512]{1,0:T(8,128)(2,1)}, u32[]{:S(2)}, u32[]{:S(2)}) collective-permute-start(bf16[32,512]{1,0:T(8,128)(2,1)} %copy-done.14), channel_id=1, source_target_pairs={{8,0},{9,1},{10,2},{11,3},{12,4},{13,5},{14,6},{15,7},{16,8},{17,9... | collective-permute-start | bytes 98312 | tf_op jit(solution)/shard_map/ppermute | solution.py:51
  112.4 6.5 %all-to-all-done.2 = bf16[8,32,512]{2,1,0:T(8,128)(2,1)S(1)} async-done(((bf16[8,32,512]{2,1,0:T(8,128)(2,1)}), bf16[8,32,512]{2,1,0:T(8,128)(2,1)S(1)}, u32[]{:S(2)}, u32[]{:S(2)}) %all-to-all-start.2) | async-done | bytes 262176 | tf_op jit(solution)/shard_map/all_to_all | solution.py:120
  118.9 1.7 %fusion.27 = f32[32,512]{1,0:T(8,128)S(1)} fusion(f32[1,512,512]{2,1,0:T(8,128)} %param.11, f32[32,512]{1,0:T(8,128)S(1)} %convert_reduce_fusion, f32[32,512]{1,0:T(8,128)S(1)} %bitcast.87, bf16[32,512]{1,0:T(8,128)(2,1)} %collective-permute-done.12, f32[512]{0:T(512)S(1)} %copy-done.15), kind=kOutput, calls=%fused_computation.36 | convolution fusion | flops 50397184 | bytes 1280000 | tf_op jit(solution)/shard_map/dot_general | solution.py:55
  120.8 1.2 collective-permute-done.13
  123.1 3.4 %collective-permute-done.14 = bf16[32,512]{1,0:T(8,128)(2,1)S(1)} collective-permute-done((bf16[32,512]{1,0:T(8,128)(2,1)S(1)}, bf16[32,512]{1,0:T(8,128)(2,1)S(1)}, u32[]{:S(2)}, u32[]{:S(2)}) %collective-permute-start.14) | collective-permute-done | bytes 32800 | tf_op jit(solution)/shard_map/ppermute | solution.py:51
  127.9 0.8 collective-permute-start.16
  129.1 1.4 collective-permute-start.17
  130.6 9.3 %collective-permute-done.17 = bf16[32,512]{1,0:T(8,128)(2,1)S(1)} collective-permute-done((bf16[32,512]{1,0:T(8,128)(2,1)S(1)}, bf16[32,512]{1,0:T(8,128)(2,1)S(1)}, u32[]{:S(2)}, u32[]{:S(2)}) %collective-permute-start.17) | collective-permute-done | bytes 32800 | tf_op jit(solution)/shard_map/ppermute | solution.py:51
  141.1 12.8 %all_to_all.20 = bf16[8,32,512]{2,1,0:T(8,128)(2,1)S(1)} all-to-all(bf16[8,32,512]{2,1,0:T(8,128)(2,1)S(1)} %broadcast_in_dim.25), channel_id=1, replica_groups=mesh['chain_0'=4,'chain_1'=2,'chain_2'=2,'tech'=4,'blk'=2] {'tech','blk'}, dimensions={0} | all-to-all | bytes 524288 | tf_op jit(solution)/shard_map/all_to_all | solution.py:60
  154.0 1.0 copy.12
  (82 shorter events, 9.3 us)
Async XLA Ops:
  0.6 14.8 %copy-start = (f32[1,512,256]{2,1,0:T(8,128)S(1)}, f32[1,512,256]{2,1,0:T(8,128)}, u32[]{:S(2)}) copy-start(f32[1,512,256]{2,1,0:T(8,128)} %param.13) | copy-start | bytes 1572868
  0.6 4.8 %copy-start.13 = (bf16[1,1,1536,256]{3,2,1,0:T(8,128)(2,1)S(1)}, bf16[1,1,1536,256]{3,2,1,0:T(8,128)(2,1)}, u32[]{:S(2)}) copy-start(bf16[1,1,1536,256]{3,2,1,0:T(8,128)(2,1)} %param.9) | copy-start | bytes 2359300
  0.7 21.1 %collective-permute-start = (bf16[1536,256]{1,0:T(8,128)(2,1)}, bf16[1536,256]{1,0:T(8,128)(2,1)S(1)}, u32[]{:S(2)}, u32[]{:S(2)}) collective-permute-start(bf16[1536,256]{1,0:T(8,128)(2,1)} %bitcast.85), channel_id=1, source_target_pairs={{0,1},{1,0},{2,3},{3,2},{4,5},{5,4},{6,7},{7,6},{8,9},{9,8},{10,11... | collective-permute-start | bytes 2359304 | tf_op jit(solution)/shard_map/ppermute | solution.py:51
  5.3 22.3 %collective-permute-start.1 = (f32[512,512]{1,0:T(8,128)S(1)}, f32[512,512]{1,0:T(8,128)}, u32[]{:S(2)}, u32[]{:S(2)}) collective-permute-start(f32[512,512]{1,0:T(8,128)S(1)} %bitcast_multiply_fusion), channel_id=1, source_target_pairs={{0,8},{1,9},{2,10},{3,11},{4,12},{5,13},{6,14},{7,15},{8,0},{9,1},... | collective-permute-start | bytes 3145736 | tf_op jit(solution)/shard_map/ppermute | solution.py:51
  10.3 4.8 %copy-start.16 = (s32[1,1,512]{2,1,0:T(1,128)S(1)}, s32[1,1,512]{2,1,0:T(1,128)}, u32[]{:S(2)}) copy-start(s32[1,1,512]{2,1,0:T(1,128)} %param.10) | copy-start | bytes 6148
  15.7 10.6 %copy-start.1 = (bf16[1,1,1536,512]{3,2,1,0:T(8,128)(2,1)S(1)}, bf16[1,1,1536,512]{3,2,1,0:T(8,128)(2,1)}, u32[]{:S(2)}) copy-start(bf16[1,1,1536,512]{3,2,1,0:T(8,128)(2,1)} %param.8) | copy-start | bytes 4718596
  21.7 4.5 %copy-start.17 = (bf16[1536,256]{1,0:T(8,128)(2,1)}, bf16[1536,256]{1,0:T(8,128)(2,1)S(1)}, u32[]{:S(2)}) copy-start(bf16[1536,256]{1,0:T(8,128)(2,1)S(1)} %collective-permute-done) | copy-start | bytes 2359300
  26.3 1.3 copy-start.3
  26.3 1.3 copy-start.15
  29.0 2.1 %copy-start.4 = (f32[512,512]{1,0:T(8,128)}, f32[512,512]{1,0:T(8,128)S(1)}, u32[]{:S(2)}) copy-start(f32[512,512]{1,0:T(8,128)S(1)} %get-tuple-element.22) | copy-start | bytes 3145732
  29.0 2.1 %copy-start.7 = (f32[512,512]{1,0:T(8,128)}, f32[512,512]{1,0:T(8,128)S(1)}, u32[]{:S(2)}) copy-start(f32[512,512]{1,0:T(8,128)S(1)} %get-tuple-element.21) | copy-start | bytes 3145732
  31.1 15.4 %all-to-all-start = ((bf16[8,32,512]{2,1,0:T(8,128)(2,1)}), bf16[8,32,512]{2,1,0:T(8,128)(2,1)S(1)}, u32[]{:S(2)}, u32[]{:S(2)}) async-start(bf16[8,32,512]{2,1,0:T(8,128)(2,1)} %bitcast.8), calls=%async_computation | async-start | bytes 524288 | tf_op jit(solution)/shard_map/all_to_all | solution.py:120
  38.1 9.6 %collective-permute-start.2 = (bf16[256,512]{1,0:T(8,128)(2,1)S(1)}, bf16[256,512]{1,0:T(8,128)(2,1)}, u32[]{:S(2)}, u32[]{:S(2)}) collective-permute-start(bf16[256,512]{1,0:T(8,128)(2,1)S(1)} %dynamic-slice_convert_fusion), channel_id=1, source_target_pairs={{0,16},{1,17},{2,18},{3,19},{4,20},{5,21},{6,22},{7,23},{8,24},{9,... | collective-permute-start | bytes 786440 | tf_op jit(solution)/shard_map/ppermute | solution.py:51
  46.5 2.9 %copy-start.8 = (f32[512,512]{1,0:T(8,128)S(1)}, f32[512,512]{1,0:T(8,128)}, u32[]{:S(2)}) copy-start(f32[512,512]{1,0:T(8,128)} %copy-done.7) | copy-start | bytes 3145732
  48.0 1.3 collective-permute-start.3
  48.1 2.5 %collective-permute-start.5 = (bf16[256,512]{1,0:T(8,128)(2,1)}, bf16[256,512]{1,0:T(8,128)(2,1)S(1)}, u32[]{:S(2)}, u32[]{:S(2)}) collective-permute-start(bf16[256,512]{1,0:T(8,128)(2,1)} %collective-permute-done.2), channel_id=1, source_target_pairs={{0,8},{1,9},{2,10},{3,11},{4,12},{5,13},{6,14},{7,15},{8,0},{9,1},... | collective-permute-start | bytes 786440 | tf_op jit(solution)/shard_map/ppermute | solution.py:51
  49.8 4.0 %collective-permute-start.4 = (bf16[32,512]{1,0:T(8,128)(2,1)S(1)}, bf16[32,512]{1,0:T(8,128)(2,1)S(1)}, u32[]{:S(2)}, u32[]{:S(2)}) collective-permute-start(bf16[32,512]{1,0:T(8,128)(2,1)S(1)} %get-tuple-element.34), channel_id=1, source_target_pairs={{0,16},{1,17},{2,18},{3,19},{4,20},{5,21},{6,22},{7,23},{8,24},{9,... | collective-permute-start | bytes 98312 | tf_op jit(solution)/shard_map/ppermute | solution.py:51
  54.2 0.7 collective-permute-start.6
  55.2 13.1 %copy-start.10 = (f32[512,512]{1,0:T(8,128)S(1)}, f32[512,512]{1,0:T(8,128)}, u32[]{:S(2)}) copy-start(f32[512,512]{1,0:T(8,128)} %get-tuple-element.25) | copy-start | bytes 3145732
  55.2 0.8 collective-permute-start.7
  56.5 12.3 %copy-start.5 = (f32[512,512]{1,0:T(8,128)S(1)}, f32[512,512]{1,0:T(8,128)}, u32[]{:S(2)}) copy-start(f32[512,512]{1,0:T(8,128)} %copy-done.4) | copy-start | bytes 3145732
  56.5 11.4 %collective-permute-start.8 = (bf16[32,512]{1,0:T(8,128)(2,1)S(1)}, bf16[32,512]{1,0:T(8,128)(2,1)S(1)}, u32[]{:S(2)}, u32[]{:S(2)}) collective-permute-start(bf16[32,512]{1,0:T(8,128)(2,1)S(1)} %fusion.24), channel_id=1, source_target_pairs={{64,96},{65,97},{66,98},{67,99},{68,100},{69,101},{70,102},{71,103... | collective-permute-start | bytes 98312 | tf_op jit(solution)/shard_map/ppermute | solution.py:51
  59.5 33.2 %collective-permute-start.9 = (bf16[192,512]{1,0:T(8,128)(2,1)}, bf16[192,512]{1,0:T(8,128)(2,1)}, u32[]{:S(2)}, u32[]{:S(2)}) collective-permute-start(bf16[192,512]{1,0:T(8,128)(2,1)} %slice_bitcast_fusion.1), channel_id=1, source_target_pairs={{0,1},{1,0},{2,3},{3,2},{4,5},{5,4},{6,7},{7,6},{8,9},{9,8},{10,11... | collective-permute-start | bytes 589832 | tf_op jit(solution)/shard_map/ppermute | solution.py:51
  69.1 0.7 copy-start.14
  69.9 15.3 %all-to-all-start.1 = ((bf16[8,32,512]{2,1,0:T(8,128)(2,1)}), bf16[8,32,512]{2,1,0:T(8,128)(2,1)S(1)}, u32[]{:S(2)}, u32[]{:S(2)}) async-start(bf16[8,32,512]{2,1,0:T(8,128)(2,1)} %broadcast_in_dim.23), calls=%async_computation.1 | async-start | bytes 524288 | tf_op jit(solution)/shard_map/all_to_all | solution.py:60
  78.6 17.5 %collective-permute-start.10 = (bf16[512,512]{1,0:T(8,128)(2,1)}, bf16[512,512]{1,0:T(8,128)(2,1)}, u32[]{:S(2)}, u32[]{:S(2)}) collective-permute-start(bf16[512,512]{1,0:T(8,128)(2,1)} %slice_bitcast_fusion), channel_id=1, source_target_pairs={{0,1},{1,0},{2,3},{3,2},{4,5},{5,4},{6,7},{7,6},{8,9},{9,8},{10,11... | collective-permute-start | bytes 1572872 | tf_op jit(solution)/shard_map/ppermute | solution.py:51
  87.4 14.1 %slice-start = ((s8[4718592]{0:T(1024)(128)(4,1)}), s8[4194304]{0:T(1024)(128)(4,1)S(1)}, s32[]{:S(2)}) async-start(s8[4718592]{0:T(1024)(128)(4,1)} %bitcast.78), calls=%async_computation.4 | async-start | bytes 8388608
  87.5 14.0 %slice-start.1 = ((s8[4718592]{0:T(1024)(128)(4,1)}), s8[524288]{0:T(1024)(128)(4,1)S(1)}, s32[]{:S(2)}) async-start(s8[4718592]{0:T(1024)(128)(4,1)} %bitcast.78), calls=%async_computation.5 | async-start | bytes 1048576
  87.5 14.0 %collective-permute-start.11 = (bf16[832,256]{1,0:T(8,128)(2,1)S(1)}, bf16[832,256]{1,0:T(8,128)(2,1)S(1)}, u32[]{:S(2)}, u32[]{:S(2)}) collective-permute-start(bf16[832,256]{1,0:T(8,128)(2,1)S(1)} %slice.25), channel_id=1, source_target_pairs={{0,1},{1,0},{2,3},{3,2},{4,5},{5,4},{6,7},{7,6},{8,9},{9,8},{10,11... | collective-permute-start | bytes 1277960 | tf_op jit(solution)/shard_map/ppermute | solution.py:51
  97.8 5.2 %copy-start.2 = (bf16[1,1,1536,512]{3,2,1,0:T(8,128)(2,1)S(1)}, bf16[1,1,1536,512]{3,2,1,0:T(8,128)(2,1)}, u32[]{:S(2)}) copy-start(bf16[1,1,1536,512]{3,2,1,0:T(8,128)(2,1)} %param.8) | copy-start | bytes 4718596
  103.0 1.3 copy-start.12
  104.3 14.6 %all-to-all-start.2 = ((bf16[8,32,512]{2,1,0:T(8,128)(2,1)}), bf16[8,32,512]{2,1,0:T(8,128)(2,1)S(1)}, u32[]{:S(2)}, u32[]{:S(2)}) async-start(bf16[8,32,512]{2,1,0:T(8,128)(2,1)} %bitcast.84), calls=%async_computation.2 | async-start | bytes 524288 | tf_op jit(solution)/shard_map/all_to_all | solution.py:120
  110.5 8.5 %collective-permute-start.12 = (bf16[32,512]{1,0:T(8,128)(2,1)}, bf16[32,512]{1,0:T(8,128)(2,1)}, u32[]{:S(2)}, u32[]{:S(2)}) collective-permute-start(bf16[32,512]{1,0:T(8,128)(2,1)} %copy-done.14), channel_id=1, source_target_pairs={{8,0},{9,1},{10,2},{11,3},{12,4},{13,5},{14,6},{15,7},{16,8},{17,9... | collective-permute-start | bytes 98312 | tf_op jit(solution)/shard_map/ppermute | solution.py:51
  118.9 3.1 %copy-start.9 = (f32[512,512]{1,0:T(8,128)S(1)}, f32[512,512]{1,0:T(8,128)}, u32[]{:S(2)}) copy-start(f32[512,512]{1,0:T(8,128)} %copy-done.7) | copy-start | bytes 3145732
  120.7 1.3 collective-permute-start.13
  122.5 4.0 %collective-permute-start.14 = (bf16[32,512]{1,0:T(8,128)(2,1)S(1)}, bf16[32,512]{1,0:T(8,128)(2,1)S(1)}, u32[]{:S(2)}, u32[]{:S(2)}) collective-permute-start(bf16[32,512]{1,0:T(8,128)(2,1)S(1)} %get-tuple-element.38), channel_id=1, source_target_pairs={{0,16},{1,17},{2,18},{3,19},{4,20},{5,21},{6,22},{7,23},{8,24},{9,... | collective-permute-start | bytes 98312 | tf_op jit(solution)/shard_map/ppermute | solution.py:51
  126.9 0.7 collective-permute-start.15
  127.9 12.4 %copy-start.11 = (f32[512,512]{1,0:T(8,128)S(1)}, f32[512,512]{1,0:T(8,128)}, u32[]{:S(2)}) copy-start(f32[512,512]{1,0:T(8,128)} %get-tuple-element.25) | copy-start | bytes 3145732
  127.9 0.8 collective-permute-start.16
  129.1 11.6 %copy-start.6 = (f32[512,512]{1,0:T(8,128)S(1)}, f32[512,512]{1,0:T(8,128)}, u32[]{:S(2)}) copy-start(f32[512,512]{1,0:T(8,128)} %copy-done.4) | copy-start | bytes 3145732
  129.1 10.7 %collective-permute-start.17 = (bf16[32,512]{1,0:T(8,128)(2,1)S(1)}, bf16[32,512]{1,0:T(8,128)(2,1)S(1)}, u32[]{:S(2)}, u32[]{:S(2)}) collective-permute-start(bf16[32,512]{1,0:T(8,128)(2,1)S(1)} %fusion.26), channel_id=1, source_target_pairs={{64,96},{65,97},{66,98},{67,99},{68,100},{69,101},{70,102},{71,103... | collective-permute-start | bytes 98312 | tf_op jit(solution)/shard_map/ppermute | solution.py:51
